TPU v7x, 32 devices: a whole 2x2x4 slice. The times are simulated.
32 devices in a mesh: row: 8 (over y, x, core), col: 4 (over z).
Axes of the slice: x: 2, y: 2, z: 4, core: 2. Of those that a mesh axis runs over, the one named last changes fastest.
Arguments:
- tokens: bfloat16 [1024, 8192], P('row', 'col'), may hold values from -200 to 200
- norm_gain: float32 [8192], P('col'), may hold values from 0.1 to 1.9
- gate_weight: bfloat16 [8192, 28672], P('col', 'row'), may hold values from -0.0625 to 0.0625
- up_weight: bfloat16 [8192, 28672], P('col', 'row'), may hold values from -0.0625 to 0.0625
- down_weight: bfloat16 [28672, 8192], P('row', 'col'), may hold values from -0.03125 to 0.03125
Outputs:
- mixed: bfloat16 [1024, 8192], P('row', 'col')
All inputs are finite; a program needn't handle non-finite values.
Results may differ from a plain program's by a relative error of at most 0.028.
Values may be sent and summed in bfloat16 or wider, within the bound.
No kernel may reach another device: no remote copies, remote signals or barrier semaphores. Data moves between devices by JAX's collectives and lax.ppermute only.
A program may use at most 128 MiB of HBM per device.

v0:
```python
import jax
import jax.numpy as jnp
from jax import lax
from jax.sharding import PartitionSpec as P

D = 8192


def apply_norm(values, squares, norm_gain):
    scale = lax.rsqrt(squares / D + 1e-05)
    return (values.astype(jnp.float32) * scale[:, None] * norm_gain[None, :]).astype(jnp.bfloat16)


def body(tokens, norm_gain, gate_weight, up_weight, down_weight):
    own = tokens.astype(jnp.float32)
    squares = lax.psum(jnp.sum(own * own, axis=1), "col")
    normed = apply_norm(tokens, squares, norm_gain)
    normed_all = lax.all_gather(normed, "row", axis=0, tiled=True)
    hidden_width = gate_weight.shape[1]
    picked = normed_all
    gate_term = jnp.dot(picked, gate_weight, preferred_element_type=jnp.float32)
    up_term = jnp.dot(picked, up_weight, preferred_element_type=jnp.float32)
    sums = lax.psum_scatter(
        jnp.concatenate([gate_term, up_term], axis=1).astype(jnp.bfloat16),
        "col",
        scatter_dimension=0,
        tiled=True,
    ).astype(jnp.float32)
    hidden = (jax.nn.silu(sums[:, :hidden_width]) * sums[:, hidden_width:]).astype(jnp.bfloat16)
    hidden_all = lax.all_gather(hidden, "col", axis=0, tiled=True)
    picked = hidden_all
    return lax.psum_scatter(
        jnp.dot(picked, down_weight, preferred_element_type=jnp.float32).astype(jnp.bfloat16),
        "row",
        scatter_dimension=0,
        tiled=True,
    )


def solution(mesh):
    placed = (P("row", "col"), P("col"), P("col", "row"), P("col", "row"), P("row", "col"))
    return jax.shard_map(
        body, mesh=mesh, in_specs=placed, out_specs=P("row", "col"), check_vma=False
    )
```

profile of v0, /device:TPU:0, one launch (start us, length us, event | category | flops | bytes accessed | tf_op | source)
XLA Modules:
  0.0 569.6 jit_solution(4243282940319229018)
XLA Ops:
  6.5 0.0 all-gather.3.cloned.1.call-start
  6.5 1.2 fusion.1
  7.8 13.5 %psum.7 = f32[128]{0:T(128)S(1)} all-reduce(f32[128]{0:T(128)S(1)} %fusion.1), channel_id=1, replica_groups=mesh['row'=8,'col'=4] {'col'}, use_global_device_ids=true, to_apply=%region_1.0 | all-reduce | flops 128 | bytes 1024 | tf_op jit(solution)/shard_map/psum | solution.py:16
  21.3 2.0 fusion.3
  23.3 0.0 all-gather.3.cloned.1.call-update
  23.3 0.0 reduce-scatter.3.cloned.1.call-start
  23.4 34.9 %all-gather.3.cloned.1.call-done = bf16[1024,2048]{1,0:T(8,128)(2,1)} async-done(((bf16[128,2048]{1,0:T(8,128)(2,1)}), bf16[1024,2048]{1,0:T(8,128)(2,1)}) %all-gather.3.cloned.1.call-update) | async-done | bytes 4194320 | tf_op jit(solution)/shard_map/all_gather | solution.py:18
  58.3 0.0 copy-start
  58.3 21.9 %convolution_convert_fusion = bf16[1024,3584]{1,0:T(8,128)(2,1)S(1)} fusion(bf16[1024,2048]{1,0:T(8,128)(2,1)} %all-gather.3.cloned.1.call-done, bf16[2048,3584]{1,0:T(8,128)(2,1)} %param.8), kind=kOutput, calls=%fused_computation.1 | convolution fusion | flops 15036055552 | bytes 26214400 | tf_op jit(solution)/shard_map/dot_general | solution.py:22
  80.1 0.0 copy-done
  80.1 18.7 %convolution_convert_fusion.1 = bf16[1024,3584]{1,0:T(8,128)(2,1)S(1)} fusion(bf16[1024,2048]{1,0:T(8,128)(2,1)S(1)} %copy-done, bf16[2048,3584]{1,0:T(8,128)(2,1)} %param.7), kind=kOutput, calls=%fused_computation.2 | convolution fusion | flops 15036055552 | bytes 26214400 | tf_op jit(solution)/shard_map/dot_general | solution.py:21
  98.8 8.7 %pad_maximum_fusion = bf16[1024,7168]{1,0:T(8,128)(2,1)} fusion(bf16[1024,3584]{1,0:T(8,128)(2,1)S(1)} %convolution_convert_fusion, bf16[1024,3584]{1,0:T(8,128)(2,1)S(1)} %convolution_convert_fusion.1), kind=kLoop, calls=%fused_computation | loop fusion | flops 29360128 | bytes 29360128 | tf_op jit(solution)/shard_map/concatenate | solution.py:24
  107.5 0.0 reduce-scatter.3.cloned.1.call-update
  107.6 0.2 all-gather.5.cloned.1.call-start
  107.8 245.7 %reduce-scatter.3.cloned.1.call-done = bf16[256,7168]{1,0:T(8,128)(2,1)} async-done(((bf16[1024,7168]{1,0:T(8,128)(2,1)}), bf16[256,7168]{1,0:T(8,128)(2,1)}) %reduce-scatter.3.cloned.1.call-update) | async-done | bytes 3670032 | tf_op jit(solution)/shard_map/reduce_scatter | solution.py:23
  353.4 2.9 convert_element_type.19
  356.3 2.4 fusion
  358.8 0.0 all-gather.5.cloned.1.call-update
  358.8 0.0 reduce-scatter.5.cloned.1.call-start
  358.9 133.6 %all-gather.5.cloned.1.call-done = bf16[1024,3584]{1,0:T(8,128)(2,1)} async-done(((bf16[256,3584]{1,0:T(8,128)(2,1)}), bf16[1024,3584]{1,0:T(8,128)(2,1)}) %all-gather.5.cloned.1.call-update) | async-done | bytes 7340048 | tf_op jit(solution)/shard_map/all_gather | solution.py:30
  492.5 21.1 %convolution_convert_fusion.2 = bf16[1024,2048]{1,0:T(8,128)(2,1)} fusion(bf16[1024,3584]{1,0:T(8,128)(2,1)} %all-gather.5.cloned.1.call-done, bf16[3584,2048]{1,0:T(8,128)(2,1)} %param.9), kind=kOutput, calls=%fused_computation.3 | convolution fusion | flops 15034482688 | bytes 26214400 | tf_op jit(solution)/shard_map/dot_general | solution.py:33
  513.5 0.0 reduce-scatter.5.cloned.1.call-update
  513.5 49.5 %reduce-scatter.5.cloned.1.call-done = bf16[128,2048]{1,0:T(8,128)(2,1)} async-done(((bf16[1024,2048]{1,0:T(8,128)(2,1)}), bf16[128,2048]{1,0:T(8,128)(2,1)}) %reduce-scatter.5.cloned.1.call-update) | async-done | bytes 524304 | tf_op jit(solution)/shard_map/reduce_scatter | solution.py:32
  (1 shorter events, 0.0 us)
Async XLA Ops:
  6.5 51.7 %all-gather.3.cloned.1.call-start = ((), (), s32[]{:S(2)}) async-start(), calls=%async_computation.2 | async-start | bytes 4718592 | tf_op jit(solution)/shard_map/all_gather | solution.py:18
  23.3 330.1 %reduce-scatter.3.cloned.1.call-start = ((), (), s32[]{:S(2)}) async-start(), calls=%async_computation.3 | async-start | bytes 18350080 | tf_op jit(solution)/shard_map/reduce_scatter | solution.py:23
  58.3 21.9 %copy-start = (bf16[1024,2048]{1,0:T(8,128)(2,1)S(1)}, bf16[1024,2048]{1,0:T(8,128)(2,1)}, u32[]{:S(2)}) copy-start(bf16[1024,2048]{1,0:T(8,128)(2,1)} %all-gather.3.cloned.1.call-done) | copy-start | bytes 12582916
  107.6 384.9 %all-gather.5.cloned.1.call-start = ((), (), s32[]{:S(2)}) async-start(), calls=%async_computation.4 | async-start | bytes 9175040 | tf_op jit(solution)/shard_map/all_gather | solution.py:30
  358.8 204.2 %reduce-scatter.5.cloned.1.call-start = ((), (), s32[]{:S(2)}) async-start(), calls=%async_computation.5 | async-start | bytes 4718592 | tf_op jit(solution)/shard_map/reduce_scatter | solution.py:32
Sparse Core Ops, SparseCore 0:
  23.4 34.7 all-gather.2
  107.7 245.7 reduce-scatter.2
  358.9 133.4 all-gather.4
  513.7 49.3 reduce-scatter.4
where the time goes:
time: 570 us
  waiting for transfers between devices  464 us (81%)
  matrix products  61.6 us (11%)
  other arithmetic  17.3 us (3%)
  blocking collectives  13.5 us (2%)
  between operations  13.2 us (2%)
    reduce_scatter x1, waiting for transfers between devices, body(): lax.psum_scatter(jnp.concatenate([gate_term, up_term], axis=1).astype(jnp...  246 us
    all_gather x1, waiting for transfers between devices, body(): hidden_all = lax.all_gather(hidden, 'col', axis=0, tiled=True)  134 us
    reduce_scatter x1, waiting for transfers between devices, body(): lax.psum_scatter(jnp.dot(picked, down_weight, preferred_element_type=jnp....  49.5 us
    all_gather x1, waiting for transfers between devices, body(): normed_all = lax.all_gather(normed, 'row', axis=0, tiled=True)  34.9 us
    dot_general x1, matrix products, body(): up_term = jnp.dot(picked, up_weight, preferred_element_type=jnp.float32)  21.9 us
    dot_general x1, matrix products, body(): jnp.dot(picked, down_weight, preferred_element_type=jnp.float32)  21.1 us
    dot_general x1, matrix products, body(): gate_term = jnp.dot(picked, gate_weight, preferred_element_type=jnp.float32)  18.7 us
    psum x1, blocking collectives, body(): squares = lax.psum(jnp.sum(own * own, axis=1), 'col')  13.5 us
  transfers between devices with their start and end apart: 4, of which 4 were waited for; matrix products, arithmetic and copies ran while one was open for 0% of the time, Pallas kernels for 0%

commit v1 on v0

v1 whole, which is shorter than its diff:
```python
import functools

import jax
import jax.numpy as jnp
from jax import lax
from jax.experimental import pallas as pl
from jax.experimental.pallas import tpu as pltpu
from jax.sharding import PartitionSpec as P


FIRST = (2, 2)
SECOND = (4, 3)
MIDDLE = (4, 3)
LAST = (2, 1)
AHEAD = 3
ROW_TILE = 32
KERNEL_VMEM = 52 * 2**20
SMALL_VMEM = 8 * 2**20


HBM = pl.BlockSpec(memory_space=pltpu.HBM)
VMEM = pl.BlockSpec(memory_space=pltpu.VMEM)
SMEM = pl.BlockSpec(memory_space=pltpu.SMEM)
ANY = pl.BlockSpec(memory_space=pl.ANY)


def gate_up_kernel(blocks, start, unit, off_ref, x_ref, gate_hbm, up_hbm, far_ref, near_ref):
    def step(gate_ref, up_ref):
        i = pl.program_id(0)
        x = x_ref[...]
        gate = jnp.dot(x, gate_ref[...], preferred_element_type=jnp.float32).astype(jnp.bfloat16)
        up = jnp.dot(x, up_ref[...], preferred_element_type=jnp.float32).astype(jnp.bfloat16)

        def write(ref, u):
            at = pl.multiple_of(2 * unit * u, 2 * unit)
            ref[:, pl.ds(at, unit)] = gate
            ref[:, pl.ds(at + unit, unit)] = up

        pl.when(i < blocks)(lambda: write(far_ref, i))
        pl.when(i >= blocks)(lambda: write(near_ref, i - blocks))

    def weight_at(i):
        return 0, off_ref[i // blocks] + start + i - (i // blocks) * blocks

    weight = pl.BlockSpec((x_ref.shape[1], unit), weight_at)
    pltpu.emit_pipeline(step, grid=(2 * blocks,), in_specs=[weight, weight])(gate_hbm, up_hbm)


def gate_up(x, gate_weight, up_weight, offsets, start, blocks, unit):
    rows, depth = x.shape
    shape = jax.ShapeDtypeStruct((rows, 2 * blocks * unit), jnp.bfloat16)
    return pl.pallas_call(
        functools.partial(gate_up_kernel, blocks, start, unit),
        in_specs=[SMEM, VMEM, HBM, HBM],
        out_specs=[VMEM, VMEM],
        out_shape=[shape, shape],
        compiler_params=pltpu.CompilerParams(vmem_limit_bytes=KERNEL_VMEM),
        cost_estimate=pl.CostEstimate(
            flops=8 * rows * depth * blocks * unit,
            bytes_accessed=8 * depth * blocks * unit,
            transcendentals=0,
        ),
    )(offsets, x, gate_weight, up_weight)


def down_kernel(steps, starts, places, unit, n_roles, has_total, off_ref, weight_hbm, *refs):
    out_ref, acc_ref = refs[-2:]
    rows, width = out_ref.shape
    count = sum(size for _, _, _, size in steps)
    acc_ref[...] = refs[-3][...] if has_total else jnp.zeros_like(acc_ref)

    def weight_at(k):
        index = 0
        for flow, chunk, first, size in steps:
            index = jnp.where(k >= first, off_ref[1 - flow] + starts[chunk] + k - first, index)
        return index, 0

    def run(role):
        def step(weight_ref, *pieces):
            k = pl.program_id(0)
            for (flow, chunk, first, size), ref in zip(steps, pieces):
                @pl.when((k >= first) & (k < first + size))
                def _():
                    acc_ref[...] += jnp.dot(ref[...], weight_ref[...], preferred_element_type=jnp.float32)

        specs, operands = [pl.BlockSpec((unit, width), weight_at)], [weight_hbm]
        for flow, chunk, first, size in steps:
            index = (2 * chunk + flow) * n_roles + role
            at = places[index]
            specs.append(pl.BlockSpec(
                (rows, unit),
                lambda k, at=at, first=first, size=size: (0, at + jnp.clip(k - first, 0, size - 1)),
            ))
            operands.append(refs[index])
        pltpu.emit_pipeline(step, grid=(count,), in_specs=specs)(*operands)

    for role in range(n_roles):
        pl.when(off_ref[2] == role)(functools.partial(run, role))
    out_ref[...] = acc_ref[...].astype(out_ref.dtype)


def down(group, weight, offsets, unit, total, dtype):
    n_roles = len(group[0][2])
    rows, width = group[0][2][0][0].shape[0], weight.shape[1]
    steps, at = [], 0
    for flow in range(2):
        for chunk, (_, size, _, _) in enumerate(group):
            steps.append((flow, chunk, at, size))
            at += size
    pieces = [piece for chunk in group for flow in range(2) for piece in chunk[2 + flow]]
    starts = [chunk[0] for chunk in group]
    extra = () if total is None else (total,)
    return pl.pallas_call(
        functools.partial(
            down_kernel, steps, starts, [place for _, place in pieces], unit, n_roles, total is not None
        ),
        in_specs=[SMEM, HBM] + [ANY] * len(pieces) + [VMEM for _ in extra],
        out_specs=VMEM,
        scratch_shapes=[pltpu.VMEM((rows, width), jnp.float32)],
        out_shape=jax.ShapeDtypeStruct((rows, width), dtype),
        compiler_params=pltpu.CompilerParams(vmem_limit_bytes=KERNEL_VMEM),
        cost_estimate=pl.CostEstimate(
            flops=2 * rows * width * at * unit,
            bytes_accessed=2 * width * at * unit,
            transcendentals=0,
        ),
    )(offsets, weight, *[message for message, _ in pieces], *extra)


def exchange_kernel(jobs, unit, n_in, role_ref, *refs):
    ins, outs = refs[:n_in], refs[n_in:]
    role = role_ref[2]

    def columns(place, size):
        return slice(place * unit, (place + size) * unit)

    def write(out, items, r):
        here = pl.ds(pl.multiple_of(r * ROW_TILE, ROW_TILE), ROW_TILE)
        for kind, place, size, part, came, came_at, scale in items:
            if kind == "sum":
                value = ins[part][here, :]
                if came is not None:
                    value = value.astype(jnp.float32) + ins[came][here, columns(came_at, 2 * size)].astype(jnp.float32)
                out[here, columns(place, 2 * size)] = value.astype(jnp.bfloat16)
            elif kind == "pass":
                out[here, columns(place, size)] = ins[came][here, columns(came_at, size)]
            else:
                for u in range(size):
                    def total(at):
                        both = ins[part][here, columns(at, 1)].astype(jnp.float32)
                        both += ins[came][here, columns(came_at + at, 1)].astype(jnp.float32)
                        return both * ins[scale][here, :]

                    gate, up = total(2 * u), total(2 * u + 1)
                    out[here, columns(place + u, 1)] = (jax.nn.silu(gate) * up).astype(jnp.bfloat16)

    roles = sorted({r for by_role in jobs for r, _ in by_role})
    for which in roles:
        @pl.when(role == which)
        def _():
            @pl.loop(0, outs[0].shape[0] // ROW_TILE)
            def _(r):
                for out, by_role in zip(outs, jobs):
                    for other, items in by_role:
                        if other == which:
                            write(out, items, r)


def exchange(jobs, widths, operands, offsets, unit):
    rows = operands[0].shape[0]
    moved = sum(a.size * a.dtype.itemsize for a in operands) + 2 * rows * sum(widths) * unit
    return pl.pallas_call(
        functools.partial(exchange_kernel, jobs, unit, len(operands)),
        in_specs=[SMEM] + [VMEM] * len(operands),
        out_specs=[VMEM] * len(widths),
        out_shape=[jax.ShapeDtypeStruct((rows, width * unit), jnp.bfloat16) for width in widths],
        compiler_params=pltpu.CompilerParams(vmem_limit_bytes=SMALL_VMEM),
        cost_estimate=pl.CostEstimate(flops=moved, bytes_accessed=moved, transcendentals=0),
    )(offsets, *operands)


def side_pairs(side, count):
    first = [z for z in range(1 - side, count - 1, 2)]
    return [(z, z + 1) for z in first] + [(z + 1, z) for z in first]


def plan(n_pair, units):
    def cut(total, sizes):
        sizes = list(sizes)
        return sizes if sum(sizes) == total else [total]

    head, tail = FIRST, LAST
    if sum(head) + sum(tail) != units:
        head, tail = (1,), (units - 1,)
    chunks, start = [], 0
    for size in head:
        chunks.append((0, start, size))
        start += size
    for pair in range(1, n_pair):
        at = 0
        for size in cut(units, SECOND if pair == 1 else MIDDLE):
            chunks.append((pair, at, size))
            at += size
    for size in tail:
        chunks.append((0, start, size))
        start += size
    return chunks


def body(n_row, n_col, tokens, norm_gain, gate_weight, up_weight, down_weight):
    col = lax.axis_index("col")
    rows, depth = tokens.shape
    half = gate_weight.shape[1] // 2
    unit = 256 if half % 256 == 0 else 128
    units = half // unit
    hops, mid = n_col - 1, n_col // 2

    low = col < mid
    far_at = jnp.where(low, units, 0)
    from_end = jnp.minimum(col, n_col - 1 - col)
    offsets = jnp.stack([far_at, units - far_at, from_end]).astype(jnp.int32)

    n_pair = n_row // 2
    chunks = plan(n_pair, units)
    count = len(chunks)
    first_use = {}
    for i, (pair, _, _) in enumerate(chunks):
        first_use.setdefault(pair, i)

    when = [[None] + [i + h for h in range(2 * hops + 1)] for i in range(count)]
    last_step = when[-1][-1]

    place, width = {}, {}
    for t in range(last_step + 1):
        for h in range(1, hops + 1):
            at = 0
            for kind, shift, scale in (("sum", 0, 2), ("hid", hops, 1)):
                for i in range(count):
                    if when[i][h + shift] == t:
                        place[kind, h, i] = at
                        at += scale * chunks[i][2]
            if at:
                width[t, h] = at

    groups, due = {}, {}
    for i, (pair, _, _) in enumerate(chunks):
        arrival = when[i][-1]
        if pair:
            arrival = max(when[j][-1] for j in range(count) if chunks[j][0] == pair)
        elif i < count // 2:
            arrival = max(when[j][-1] for j in range(count // 2) if chunks[j][0] == pair)
        groups.setdefault((arrival, pair), []).append(i)
    for arrival, pair in groups:
        due[pair] = max(due.get(pair, 0), arrival)

    def sends_of(side):
        hops_of = [(e, e + 1 if (e + 1) % 2 == side else n_col - e) for e in range(mid)]
        return [(e, h) for e, h in hops_of if h < n_col]

    def along_row(value, mask):
        return lax.ppermute(value, "row", [(r, r ^ mask) for r in range(n_row)])

    def along_col(value, mask):
        return lax.ppermute(value, "col", [(c, c ^ mask) for c in range(n_col)])

    def start_chunk(i, x):
        _, start, blocks = chunks[i]
        return gate_up(x, gate_weight, up_weight, offsets, start, blocks, unit)

    own = tokens.astype(jnp.float32)
    gained = (own * norm_gain[None, :]).astype(jnp.bfloat16)
    squares = jnp.sum(own * own, axis=1)[None, :]
    lhs = {0: jnp.concatenate([gained, along_row(gained, 1)], axis=0)}
    scales = {}

    col_masks = [1 << b for b in range(n_col.bit_length() - 1)]
    far, near, came, sent, totals, outs = {}, {}, {}, {}, {}, {}
    far[0], near[0] = start_chunk(0, lhs[0])
    carried = {}
    for t in range(last_step + 1):
        jobs, widths, sides, operands, known = [], [], [], [], {}
        messages = {}

        def operand(name, value):
            if name not in known:
                known[name] = len(operands)
                operands.append(value)
            return known[name]

        def received(h, i, shift):
            before = (when[i][h + shift], h % 2)
            return operand(before, came[before]), place["hid" if shift else "sum", h, i]

        for side in (1, 0):
            active = [(e, h) for e, h in sends_of(side) if (t, h) in width]
            if not active:
                continue
            by_role = []
            for e, h in active:
                items = []
                for i in range(count):
                    size = chunks[i][2]
                    if when[i][h] == t:
                        mine = ("far", i) if h <= mid else ("near", i)
                        part = operand(mine, (far if h <= mid else near)[i])
                        old = received(h - 1, i, 0) if h > 1 else (None, 0)
                        items.append(("sum", place["sum", h, i], size, part, *old, None))
                    if when[i][h + hops] == t and h == 1:
                        pair = chunks[i][0]
                        part, old = operand(("near", i), near[i]), received(hops, i, 0)
                        scale = operand(("scale", pair), scales[pair].reshape(2 * rows, 1))
                        items.append(("hid", place["hid", h, i], size, part, *old, scale))
                    elif when[i][h + hops] == t:
                        old = received(h - 1, i, hops)
                        items.append(("pass", place["hid", h, i], size, None, *old, None))
                by_role.append((e, items))
            only = by_role[0][1][0] if len(by_role) == len(by_role[0][1]) == 1 else None
            if only and only[0] == "sum" and only[4] is None:
                messages[side] = operands[only[3]]
            else:
                jobs.append(by_role)
                sides.append(side)
                widths.append(max(width[t, h] for _, h in active))
        if jobs:
            messages.update(zip(sides, exchange(jobs, widths, operands, offsets, unit)))

        extra = {}
        wanted = [pair for pair in range(1, n_pair) if max(0, first_use[pair] - AHEAD) == t]
        if wanted:
            extra["gained"] = lhs[0]
        if t + 1 < count:
            extra["x"] = lhs[chunks[t + 1][0]]
        if t <= len(col_masks) + 1:
            extra["squares"] = squares
        arrived = [(pair, members) for (arrival, pair), members in groups.items() if arrival == t]
        for pair, members in arrived:
            for i in members:
                for h in range(1, hops + 1):
                    key = (when[i][h + hops], h % 2)
                    extra["came", key] = came[key]
        extra.update(carried)
        carried = {}

        values = lax.optimization_barrier((list(messages.values()), list(extra.values())))
        messages, extra = dict(zip(messages, values[0])), dict(zip(extra, values[1]))
        for key in [key for key in extra if isinstance(key, tuple) and key[0] == "total"]:
            totals[key] = extra[key]
        for side, value in messages.items():
            came[t, side] = lax.ppermute(value, "col", side_pairs(side, n_col))
            sent[t, side] = value
        for pair in wanted:
            lhs[pair] = along_row(extra["gained"], 2 * pair)
        if t < len(col_masks):
            squares = extra["squares"] + along_col(extra["squares"], col_masks[t])
        elif t == len(col_masks):
            scale = lax.rsqrt(extra["squares"] / (depth * n_col) + 1e-05)
            squares = scales[0] = jnp.concatenate([scale, along_row(scale, 1)], axis=0)
        elif t == len(col_masks) + 1:
            for pair in range(1, n_pair):
                scales[pair] = along_row(extra["squares"], 2 * pair)
        if "x" in extra:
            far[t + 1], near[t + 1] = start_chunk(t + 1, extra["x"])
        for pair, members in arrived:
            group = []
            for i in members:
                def hidden(h):
                    if h == 0:
                        return sent[when[i][1 + hops], 1], place["hid", 1, i]
                    return extra["came", (when[i][h + hops], h % 2)], place["hid", h, i]

                roles = range(mid)
                group.append((
                    chunks[i][1], chunks[i][2],
                    [hidden(e) for e in roles], [hidden(n_col - 1 - e) for e in roles],
                ))
            last = due[pair] == t
            result = down(
                group, down_weight, offsets, unit, totals.pop(("total", pair), None),
                jnp.bfloat16 if last and pair else jnp.float32,
            )
            if not last:
                carried["total", pair] = result
            elif pair == 0:
                outs[pair] = result
            else:
                outs[pair] = along_row(result, 2 * pair)
    mixed = functools.reduce(jnp.add, [outs[pair].astype(jnp.float32) for pair in range(n_pair)])
    other = along_row(mixed[rows:].astype(jnp.bfloat16), 1)
    return (mixed[:rows] + other.astype(jnp.float32)).astype(jnp.bfloat16)


def solution(mesh):
    placed = (P("row", "col"), P("col"), P("col", "row"), P("col", "row"), P("row", "col"))
    n_row, n_col = mesh.shape["row"], mesh.shape["col"]
    return jax.shard_map(
        functools.partial(body, n_row, n_col),
        mesh=mesh, in_specs=placed, out_specs=P("row", "col"), check_vma=False,
    )
```

time: 570 us -> 425 us (0.75)
  waiting for transfers between devices: 464 us -> 162 us
  Pallas kernels: 0 us -> 184 us
  starting transfers between devices: 0.31 us -> 65.8 us
  matrix products: 61.6 us -> 0 us
  blocking collectives: 13.5 us -> 0 us
  between operations: 13.2 us -> 0.73 us
  other arithmetic: 17.3 us -> 5.58 us
    reduce_scatter x2 -> x0, waiting for transfers between devices: 295 us -> none  [the longest x1 246 us: body(): lax.psum_scatter(jnp.concatenate([gate_term, up_term], axis=1).astype(jnp...]
    pallas_call x0 -> x30, Pallas kernels: none -> 184 us  [the longest x10 91.4 us: gate_up(): pl.pallas_call(functools.partial(gate_up_kernel, blocks, start, unit), in...]
    all_gather x2 -> x0, waiting for transfers between devices: 168 us -> none  [the longest x1 134 us: body(): hidden_all = lax.all_gather(hidden, 'col', axis=0, tiled=True)]
    ppermute x0 -> x42, waiting for transfers between devices: none -> 162 us  [the longest x28 119 us: body(): came[t, side] = lax.ppermute(value, 'col', side_pairs(side, n_col))]
    ppermute x0 -> x42, starting transfers between devices: none -> 65.8 us  [the longest x28 51.8 us: body(): came[t, side] = lax.ppermute(value, 'col', side_pairs(side, n_col))]
    dot_general x3 -> x0, matrix products: 61.6 us -> none  [the longest x1 21.9 us: body(): up_term = jnp.dot(picked, up_weight, preferred_element_type=jnp.float32)]
    psum x1 -> x0, blocking collectives: 13.5 us -> none  [body(): squares = lax.psum(jnp.sum(own * own, axis=1), 'col')]
    concatenate x1 -> x2, other arithmetic: 8.72 us -> 1.08 us  [the longest x1 1.07 us: body(): lhs = {0: jnp.concatenate([gained, along_row(gained, 1)], axis=0)}]
  transfers between devices with their start and end apart: 4 -> 42, of which waited for: 4 -> 17; matrix products, arithmetic and copies ran while one was open for 0% -> 0% of each run, Pallas kernels for 0% -> 37%
where the time goes in v1:
time: 425 us; the launch traced here: 422 us
  Pallas kernels  184 us (43%)
  waiting for transfers between devices  162 us (38%)
  starting transfers between devices  65.8 us (15%)
  other arithmetic  5.58 us (1%)
  local copies, waits for them, and re-layouts  4.99 us (1%)
    ppermute x28, waiting for transfers between devices, body(): came[t, side] = lax.ppermute(value, 'col', side_pairs(side, n_col))  119 us
    pallas_call x10, Pallas kernels, gate_up(): pl.pallas_call(functools.partial(gate_up_kernel, blocks, start, unit), in...  91.4 us
    pallas_call x6, Pallas kernels, down(): pl.pallas_call(functools.partial(down_kernel, steps, starts, [place for _...  66.5 us
    ppermute x28, starting transfers between devices, body(): came[t, side] = lax.ppermute(value, 'col', side_pairs(side, n_col))  51.8 us
    ppermute x12, waiting for transfers between devices, along_row(): return lax.ppermute(value, 'row', [(r, r ^ mask) for r in range(n_row)])  38.1 us
    pallas_call x14, Pallas kernels, exchange(): pl.pallas_call(functools.partial(exchange_kernel, jobs, unit, len(operand...  25.8 us
    ppermute x12, starting transfers between devices, along_row(): return lax.ppermute(value, 'row', [(r, r ^ mask) for r in range(n_row)])  13.6 us
  transfers between devices with their start and end apart: 42, of which 17 were waited for; matrix products, arithmetic and copies ran while one was open for 0% of the time, Pallas kernels for 37%

profile of v1, /device:TPU:0, one launch (start us, length us, event | category | flops | bytes accessed | tf_op | source)
XLA Modules:
  0.0 422.2 jit_solution(10588866554386352813)
XLA Ops:
  1.9 1.5 collective-permute-done
  4.4 7.0 %shard_map.55 = (bf16[256,1024]{1,0:T(8,128)(2,1)S(1)}, bf16[256,1024]{1,0:T(8,128)(2,1)S(1)}) custom-call(s32[3]{0:T(128)S(1)} %pad_add_fusion.off_ref.role_ref, bf16[256,2048]{1,0:T(8,128)(2,1)} %pad_maximum_fusion.x_ref, bf16[2048,3584]{1,0:T(8,128)(2,1)} %gate_hbm.19, bf16[2048,3584]{1,0:T(8,128)(2,1)} %up_hbm.19), custom_call_target="tpu_custom_call" | custom-call | flops 2147483648 | bytes 8388608 | tf_op jit(solution)/shard_map/pallas_call | solution.py:52
  11.4 2.9 collective-permute-start.2
  14.4 1.6 collective-permute-start.1
  16.4 6.9 %shard_map.56 = (bf16[256,1024]{1,0:T(8,128)(2,1)S(1)}, bf16[256,1024]{1,0:T(8,128)(2,1)S(1)}) custom-call(s32[3]{0:T(128)S(1)} %pad_add_fusion.off_ref.role_ref, bf16[256,2048]{1,0:T(8,128)(2,1)} %pad_maximum_fusion.x_ref, bf16[2048,3584]{1,0:T(8,128)(2,1)} %gate_hbm.19, bf16[2048,3584]{1,0:T(8,128)(2,1)} %up_hbm.19), custom_call_target="tpu_custom_call" | custom-call | flops 2147483648 | bytes 8388608 | tf_op jit(solution)/shard_map/pallas_call | solution.py:52
  23.3 4.9 %collective-permute-done.3 = f32[1,128]{1,0:T(1,128)S(1)} collective-permute-done((f32[1,128]{1,0:T(1,128)S(1)}, f32[1,128]{1,0:T(1,128)S(1)}, u32[]{:S(2)}, u32[]{:S(2)}) %collective-permute-start.3) | collective-permute-done | bytes 544 | tf_op jit(solution)/shard_map/ppermute | solution.py:264
  28.7 9.1 %collective-permute-done.2.x_ref = bf16[256,2048]{1,0:T(8,128)(2,1)S(1)} collective-permute-done((bf16[256,2048]{1,0:T(8,128)(2,1)S(1)}, bf16[256,2048]{1,0:T(8,128)(2,1)S(1)}, u32[]{:S(2)}, u32[]{:S(2)}) %collective-permute-start.2) | collective-permute-done | bytes 1048608 | tf_op jit(solution)/shard_map/ppermute | solution.py:261
  38.5 4.7 %collective-permute-start.5 = (bf16[256,1024]{1,0:T(8,128)(2,1)S(1)}, bf16[256,1024]{1,0:T(8,128)(2,1)S(1)}, u32[]{:S(2)}, u32[]{:S(2)}) collective-permute-start(bf16[256,1024]{1,0:T(8,128)(2,1)S(1)} %get-tuple-element.132.refs_0_.refs_3_), channel_id=1, source_target_pairs={{0,1},{2,3},{1,0},{3,2},{4,5},{6,7},{5,4},{7,6},{8,9},{10,11},{9,8... | collective-permute-start | bytes 1572872 | tf_op jit(solution)/shard_map/ppermute | solution.py:349
  43.2 12.9 %shard_map.58 = (bf16[256,2048]{1,0:T(8,128)(2,1)S(1)}, bf16[256,2048]{1,0:T(8,128)(2,1)}) custom-call(s32[3]{0:T(128)S(1)} %pad_add_fusion.off_ref.role_ref, bf16[256,2048]{1,0:T(8,128)(2,1)} %copy-done.44, bf16[2048,3584]{1,0:T(8,128)(2,1)} %gate_hbm.19, bf16[2048,3584]{1,0:T(8,128)(2,1)} %up_hbm.19), custom_call_target="tpu_custom_call" | custom-call | flops 4294967296 | bytes 16777216 | tf_op jit(solution)/shard_map/pallas_call | solution.py:52
  56.1 1.8 shard_map.59
  57.9 2.1 collective-permute-start.7
  60.0 1.5 collective-permute-start.10
  61.5 1.4 collective-permute-start.9
  63.0 9.4 %shard_map.60 = (bf16[256,1536]{1,0:T(8,128)(2,1)S(1)}, bf16[256,1536]{1,0:T(8,128)(2,1)S(1)}) custom-call(s32[3]{0:T(128)S(1)} %pad_add_fusion.off_ref.role_ref, bf16[256,2048]{1,0:T(8,128)(2,1)} %copy-done.44, bf16[2048,3584]{1,0:T(8,128)(2,1)} %gate_hbm.19, bf16[2048,3584]{1,0:T(8,128)(2,1)} %up_hbm.19), custom_call_target="tpu_custom_call" | custom-call | flops 3221225472 | bytes 12582912 | tf_op jit(solution)/shard_map/pallas_call | solution.py:52
  73.4 8.6 %collective-permute-done.7.refs_1_ = bf16[256,2048]{1,0:T(8,128)(2,1)} collective-permute-done((bf16[256,2048]{1,0:T(8,128)(2,1)}, bf16[256,2048]{1,0:T(8,128)(2,1)}, u32[]{:S(2)}, u32[]{:S(2)}) %collective-permute-start.7) | collective-permute-done | bytes 1048608 | tf_op jit(solution)/shard_map/ppermute | solution.py:349
  83.1 2.1 shard_map.61
  85.2 1.5 collective-permute-start.11
  87.5 12.9 %shard_map.62 = (bf16[256,2048]{1,0:T(8,128)(2,1)S(1)}, bf16[256,2048]{1,0:T(8,128)(2,1)}) custom-call(s32[3]{0:T(128)S(1)} %pad_add_fusion.off_ref.role_ref, bf16[256,2048]{1,0:T(8,128)(2,1)} %collective-permute-done.10.x_ref, bf16[2048,3584]{1,0:T(8,128)(2,1)} %gate_hbm.19, bf16[2048,3584]{1,0:T(8,128)(2,1)} %up_hbm.19), custom_call_target="tpu_custom_call" | custom-call | flops 4294967296 | bytes 16777216 | tf_op jit(solution)/shard_map/pallas_call | solution.py:52
  100.3 7.9 %collective-permute-done.11.refs_1_ = bf16[256,2048]{1,0:T(8,128)(2,1)S(1)} collective-permute-done((bf16[256,2048]{1,0:T(8,128)(2,1)S(1)}, bf16[256,2048]{1,0:T(8,128)(2,1)S(1)}, u32[]{:S(2)}, u32[]{:S(2)}) %collective-permute-start.11) | collective-permute-done | bytes 1048608 | tf_op jit(solution)/shard_map/ppermute | solution.py:349
  108.3 2.8 shard_map.63
  111.1 3.5 collective-permute-start.13
  115.3 2.5 collective-permute-start.16
  118.3 19.5 %collective-permute-done.14 = f32[2,128]{1,0:T(2,128)S(1)} collective-permute-done((f32[2,128]{1,0:T(2,128)S(1)}, f32[2,128]{1,0:T(2,128)S(1)}, u32[]{:S(2)}, u32[]{:S(2)}) %collective-permute-start.14) | collective-permute-done | bytes 1056 | tf_op jit(solution)/shard_map/ppermute | solution.py:261
  138.0 9.5 %shard_map.64 = (bf16[256,1536]{1,0:T(8,128)(2,1)S(1)}, bf16[256,1536]{1,0:T(8,128)(2,1)S(1)}) custom-call(s32[3]{0:T(128)S(1)} %pad_add_fusion.off_ref.role_ref, bf16[256,2048]{1,0:T(8,128)(2,1)} %collective-permute-done.10.x_ref, bf16[2048,3584]{1,0:T(8,128)(2,1)} %gate_hbm.19, bf16[2048,3584]{1,0:T(8,128)(2,1)} %up_hbm.19), custom_call_target="tpu_custom_call" | custom-call | flops 3221225472 | bytes 12582912 | tf_op jit(solution)/shard_map/pallas_call | solution.py:52
  149.2 2.8 collective-permute-start.17
  152.8 12.9 %shard_map.66 = (bf16[256,2048]{1,0:T(8,128)(2,1)S(1)}, bf16[256,2048]{1,0:T(8,128)(2,1)}) custom-call(s32[3]{0:T(128)S(1)} %pad_add_fusion.off_ref.role_ref, bf16[256,2048]{1,0:T(8,128)(2,1)} %collective-permute-done.16.x_ref, bf16[2048,3584]{1,0:T(8,128)(2,1)} %gate_hbm.19, bf16[2048,3584]{1,0:T(8,128)(2,1)} %up_hbm.19), custom_call_target="tpu_custom_call" | custom-call | flops 4294967296 | bytes 16777216 | tf_op jit(solution)/shard_map/pallas_call | solution.py:52
  165.7 11.0 %collective-permute-done.17.refs_1_.refs_2_ = bf16[256,2560]{1,0:T(8,128)(2,1)S(1)} collective-permute-done((bf16[256,2560]{1,0:T(8,128)(2,1)S(1)}, bf16[256,2560]{1,0:T(8,128)(2,1)S(1)}, u32[]{:S(2)}, u32[]{:S(2)}) %collective-permute-start.17) | collective-permute-done | bytes 1310752 | tf_op jit(solution)/shard_map/ppermute | solution.py:349
  176.7 2.9 shard_map.67
  179.6 3.6 collective-permute-start.19
  183.2 1.7 collective-permute-start.21
  185.4 3.1 collective-permute-done.20
  189.2 9.5 %shard_map.68 = (bf16[256,1536]{1,0:T(8,128)(2,1)S(1)}, bf16[256,1536]{1,0:T(8,128)(2,1)S(1)}) custom-call(s32[3]{0:T(128)S(1)} %pad_add_fusion.off_ref.role_ref, bf16[256,2048]{1,0:T(8,128)(2,1)} %collective-permute-done.16.x_ref, bf16[2048,3584]{1,0:T(8,128)(2,1)} %gate_hbm.19, bf16[2048,3584]{1,0:T(8,128)(2,1)} %up_hbm.19), custom_call_target="tpu_custom_call" | custom-call | flops 3221225472 | bytes 12582912 | tf_op jit(solution)/shard_map/pallas_call | solution.py:52
  198.7 11.2 %collective-permute-done.19.refs_1_.refs_6_.refs_5_ = bf16[256,2816]{1,0:T(8,128)(2,1)S(1)} collective-permute-done((bf16[256,2816]{1,0:T(8,128)(2,1)}, bf16[256,2816]{1,0:T(8,128)(2,1)S(1)}, u32[]{:S(2)}, u32[]{:S(2)}) %collective-permute-start.19) | collective-permute-done | bytes 1441824 | tf_op jit(solution)/shard_map/ppermute | solution.py:349
  210.0 3.8 shard_map.69
  214.7 2.9 collective-permute-start.22
  217.6 6.9 %shard_map.70 = (bf16[256,1024]{1,0:T(8,128)(2,1)S(1)}, bf16[256,1024]{1,0:T(8,128)(2,1)S(1)}) custom-call(s32[3]{0:T(128)S(1)} %pad_add_fusion.off_ref.role_ref, bf16[256,2048]{1,0:T(8,128)(2,1)} %pad_maximum_fusion.x_ref, bf16[2048,3584]{1,0:T(8,128)(2,1)} %gate_hbm.19, bf16[2048,3584]{1,0:T(8,128)(2,1)} %up_hbm.19), custom_call_target="tpu_custom_call" | custom-call | flops 2147483648 | bytes 8388608 | tf_op jit(solution)/shard_map/pallas_call | solution.py:52
  225.3 10.0 %shard_map.72.refs_4_ = f32[256,2048]{1,0:T(8,128)} custom-call(s32[3]{0:T(128)S(1)} %pad_add_fusion.off_ref.role_ref, bf16[3584,2048]{1,0:T(8,128)(2,1)} %weight_hbm.11, bf16[256,2048]{1,0:T(8,128)(2,1)S(1)} %copy-done.42, bf16[256,2048]{1,0:T(8,128)(2,1)} %copy-done.14, bf16[256,2560]{1,0:T(8,128)(2,1)} %copy-done.5, bf16[256,2048]{1,0:T(8,128)(2,1)} %copy-done.13, ...), custom_call_target="tpu_custom_call" | custom-call | flops 2147483648 | bytes 8388608 | tf_op jit(solution)/shard_map/pallas_call | solution.py:113
  235.3 5.2 %collective-permute-done.22.refs_1_.refs_2_ = bf16[256,2560]{1,0:T(8,128)(2,1)S(1)} collective-permute-done((bf16[256,2560]{1,0:T(8,128)(2,1)S(1)}, bf16[256,2560]{1,0:T(8,128)(2,1)S(1)}, u32[]{:S(2)}, u32[]{:S(2)}) %collective-permute-start.22) | collective-permute-done | bytes 1310752 | tf_op jit(solution)/shard_map/ppermute | solution.py:349
  240.5 2.8 shard_map.71
  243.4 4.3 %collective-permute-start.24 = (bf16[256,2816]{1,0:T(8,128)(2,1)}, bf16[256,2816]{1,0:T(8,128)(2,1)S(1)}, u32[]{:S(2)}, u32[]{:S(2)}) collective-permute-start(bf16[256,2816]{1,0:T(8,128)(2,1)} %get-tuple-element.191.refs_4_), channel_id=1, source_target_pairs={{0,1},{2,3},{1,0},{3,2},{4,5},{6,7},{5,4},{7,6},{8,9},{10,11},{9,8... | collective-permute-start | bytes 4325384 | tf_op jit(solution)/shard_map/ppermute | solution.py:349
  247.7 1.8 collective-permute-start.26
  249.5 1.4 collective-permute-start.25
  250.9 3.1 collective-permute-done.25
  254.8 3.6 shard_map.73
  258.4 16.4 %collective-permute-done.24.refs_1_.refs_6_.refs_5_ = bf16[256,2816]{1,0:T(8,128)(2,1)S(1)} collective-permute-done((bf16[256,2816]{1,0:T(8,128)(2,1)}, bf16[256,2816]{1,0:T(8,128)(2,1)S(1)}, u32[]{:S(2)}, u32[]{:S(2)}) %collective-permute-start.24) | collective-permute-done | bytes 1441824 | tf_op jit(solution)/shard_map/ppermute | solution.py:349
  274.9 2.7 shard_map.74
  277.6 2.0 collective-permute-start.27
  280.3 24.9 %collective-permute-done.27.refs_1_.refs_2_ = bf16[256,2560]{1,0:T(8,128)(2,1)S(1)} collective-permute-done((bf16[256,2560]{1,0:T(8,128)(2,1)S(1)}, bf16[256,2560]{1,0:T(8,128)(2,1)S(1)}, u32[]{:S(2)}, u32[]{:S(2)}) %collective-permute-start.27) | collective-permute-done | bytes 1310752 | tf_op jit(solution)/shard_map/ppermute | solution.py:349
  306.5 2.0 collective-permute-start.29
  309.2 16.5 %collective-permute-done.29.refs_1_.refs_6_.refs_5_ = bf16[256,1792]{1,0:T(8,128)(2,1)S(1)} collective-permute-done((bf16[256,1792]{1,0:T(8,128)(2,1)S(1)}, bf16[256,1792]{1,0:T(8,128)(2,1)S(1)}, u32[]{:S(2)}, u32[]{:S(2)}) %collective-permute-start.29) | collective-permute-done | bytes 917536 | tf_op jit(solution)/shard_map/ppermute | solution.py:349
  327.1 2.0 collective-permute-start.31
  329.7 13.6 %collective-permute-done.31.refs_1_.refs_2_ = bf16[256,1536]{1,0:T(8,128)(2,1)S(1)} collective-permute-done((bf16[256,1536]{1,0:T(8,128)(2,1)S(1)}, bf16[256,1536]{1,0:T(8,128)(2,1)S(1)}, u32[]{:S(2)}, u32[]{:S(2)}) %collective-permute-start.31) | collective-permute-done | bytes 786464 | tf_op jit(solution)/shard_map/ppermute | solution.py:349
  345.9 13.9 %shard_map.82 = bf16[256,2048]{1,0:T(8,128)(2,1)S(1)} custom-call(s32[3]{0:T(128)S(1)} %pad_add_fusion.off_ref.role_ref, bf16[3584,2048]{1,0:T(8,128)(2,1)} %weight_hbm.11, bf16[256,2560]{1,0:T(8,128)(2,1)} %copy-done.36, bf16[256,2560]{1,0:T(8,128)(2,1)} %copy-done.5, bf16[256,2560]{1,0:T(8,128)(2,1)} %copy-done.7, ...), custom_call_target="tpu_custom_call" | custom-call | flops 3758096384 | bytes 14680064 | tf_op jit(solution)/shard_map/pallas_call | solution.py:113
  359.9 1.5 collective-permute-start.38
  362.1 14.9 %shard_map.83 = bf16[256,2048]{1,0:T(8,128)(2,1)} custom-call(s32[3]{0:T(128)S(1)} %pad_add_fusion.off_ref.role_ref, bf16[3584,2048]{1,0:T(8,128)(2,1)} %weight_hbm.11, bf16[256,2560]{1,0:T(8,128)(2,1)} %copy-done.37, bf16[256,2560]{1,0:T(8,128)(2,1)} %copy-done.7, bf16[256,2560]{1,0:T(8,128)(2,1)} %copy-done.6, ...), custom_call_target="tpu_custom_call" | custom-call | flops 3758096384 | bytes 14680064 | tf_op jit(solution)/shard_map/pallas_call | solution.py:113
  378.1 15.0 %shard_map.84 = bf16[256,2048]{1,0:T(8,128)(2,1)} custom-call(s32[3]{0:T(128)S(1)} %pad_add_fusion.off_ref.role_ref, bf16[3584,2048]{1,0:T(8,128)(2,1)} %weight_hbm.11, bf16[256,2560]{1,0:T(8,128)(2,1)} %copy-done.38, bf16[256,2560]{1,0:T(8,128)(2,1)} %copy-done.6, bf16[256,1536]{1,0:T(8,128)(2,1)S(1)} %collective-permute-done.31.refs_1_.refs_2_, ...), custom_call_target="tpu_custom_call" | custom-call | flops 3758096384 | bytes 14680064 | tf_op jit(solution)/shard_map/pallas_call | solution.py:113
  393.2 1.5 collective-permute-start.40
  394.7 2.3 collective-permute-start.36
  398.2 3.1 collective-permute-done.36.refs_2_
  401.4 3.2 collective-permute-start.37
  404.5 7.2 %shard_map.80.refs_4_ = f32[256,2048]{1,0:T(8,128)} custom-call(s32[3]{0:T(128)S(1)} %pad_add_fusion.off_ref.role_ref, bf16[3584,2048]{1,0:T(8,128)(2,1)} %weight_hbm.11, bf16[256,1536]{1,0:T(8,128)(2,1)S(1)} %get-tuple-element.202.refs_0_, bf16[256,1536]{1,0:T(8,128)(2,1)} %copy-done.9, bf16[256,512]{1,0:T(8,128)(2,1)S(1)} %collective-permute-done.36.refs_2_, ...), custom_call_target="tpu_custom_call" | custom-call | flops 1073741824 | bytes 4194304 | tf_op jit(solution)/shard_map/pallas_call | solution.py:113
  411.7 5.4 %shard_map.81 = f32[256,2048]{1,0:T(8,128)} custom-call(s32[3]{0:T(128)S(1)} %pad_add_fusion.off_ref.role_ref, bf16[3584,2048]{1,0:T(8,128)(2,1)} %weight_hbm.11, bf16[256,768]{1,0:T(8,128)(2,1)S(1)} %get-tuple-element.204.refs_0_, bf16[256,768]{1,0:T(8,128)(2,1)S(1)} %collective-permute-done.33.refs_1_.refs_6_, ...), custom_call_target="tpu_custom_call" | custom-call | flops 536870912 | bytes 2097152 | tf_op jit(solution)/shard_map/pallas_call | solution.py:113
  417.1 2.2 convert_add_fusion
  419.4 1.9 collective-permute-done.41
  (154 shorter events, 26.4 us)
Async XLA Ops:
  1.3 2.1 collective-permute-start
  11.4 44.7 %copy-start.30 = (bf16[256,1024]{1,0:T(8,128)(2,1)}, bf16[256,1024]{1,0:T(8,128)(2,1)S(1)}, u32[]{:S(2)}) copy-start(bf16[256,1024]{1,0:T(8,128)(2,1)S(1)} %get-tuple-element.124.refs_1_.refs_0_) | copy-start | bytes 1572868
  11.4 26.4 %collective-permute-start.2 = (bf16[256,2048]{1,0:T(8,128)(2,1)S(1)}, bf16[256,2048]{1,0:T(8,128)(2,1)S(1)}, u32[]{:S(2)}, u32[]{:S(2)}) collective-permute-start(bf16[256,2048]{1,0:T(8,128)(2,1)S(1)} %copy-done), channel_id=1, source_target_pairs={{0,8},{4,12},{8,0},{12,4},{16,24},{20,28},{24,16},{28,20},{1,9},{5... | collective-permute-start | bytes 3145736 | tf_op jit(solution)/shard_map/ppermute | solution.py:261
  14.4 13.8 %collective-permute-start.1 = (bf16[256,1024]{1,0:T(8,128)(2,1)S(1)}, bf16[256,1024]{1,0:T(8,128)(2,1)S(1)}, u32[]{:S(2)}, u32[]{:S(2)}) collective-permute-start(bf16[256,1024]{1,0:T(8,128)(2,1)S(1)} %get-tuple-element.126.refs_1_), channel_id=1, source_target_pairs={{0,1},{2,3},{1,0},{3,2},{4,5},{6,7},{5,4},{7,6},{8,9},{10,11},{9,8... | collective-permute-start | bytes 1572872 | tf_op jit(solution)/shard_map/ppermute | solution.py:349
  15.9 12.2 %collective-permute-start.3 = (f32[1,128]{1,0:T(1,128)S(1)}, f32[1,128]{1,0:T(1,128)S(1)}, u32[]{:S(2)}, u32[]{:S(2)}) collective-permute-start(f32[1,128]{1,0:T(1,128)S(1)} %bitcast.12), channel_id=1, source_target_pairs={{0,1},{1,0},{2,3},{3,2},{4,5},{5,4},{6,7},{7,6},{8,9},{9,8},{10,11... | collective-permute-start | bytes 1544 | tf_op jit(solution)/shard_map/ppermute | solution.py:264
  37.8 18.3 %collective-permute-start.4 = (bf16[256,1024]{1,0:T(8,128)(2,1)S(1)}, bf16[256,1024]{1,0:T(8,128)(2,1)S(1)}, u32[]{:S(2)}, u32[]{:S(2)}) collective-permute-start(bf16[256,1024]{1,0:T(8,128)(2,1)S(1)} %shard_map.57), channel_id=1, source_target_pairs={{1,2},{2,1},{5,6},{6,5},{9,10},{10,9},{13,14},{14,13},{17,18},{18,... | collective-permute-start | bytes 1572872 | tf_op jit(solution)/shard_map/ppermute | solution.py:349
  38.5 17.6 %collective-permute-start.5 = (bf16[256,1024]{1,0:T(8,128)(2,1)S(1)}, bf16[256,1024]{1,0:T(8,128)(2,1)S(1)}, u32[]{:S(2)}, u32[]{:S(2)}) collective-permute-start(bf16[256,1024]{1,0:T(8,128)(2,1)S(1)} %get-tuple-element.132.refs_0_.refs_3_), channel_id=1, source_target_pairs={{0,1},{2,3},{1,0},{3,2},{4,5},{6,7},{5,4},{7,6},{8,9},{10,11},{9,8... | collective-permute-start | bytes 1572872 | tf_op jit(solution)/shard_map/ppermute | solution.py:349
  43.2 12.9 %collective-permute-start.6 = (f32[1,128]{1,0:T(1,128)S(1)}, f32[1,128]{1,0:T(1,128)S(1)}, u32[]{:S(2)}, u32[]{:S(2)}) collective-permute-start(f32[1,128]{1,0:T(1,128)S(1)} %add.24), channel_id=1, source_target_pairs={{0,2},{1,3},{2,0},{3,1},{4,6},{5,7},{6,4},{7,5},{8,10},{9,11},{10,... | collective-permute-start | bytes 1544 | tf_op jit(solution)/shard_map/ppermute | solution.py:264
  57.9 24.2 %collective-permute-start.7 = (bf16[256,2048]{1,0:T(8,128)(2,1)}, bf16[256,2048]{1,0:T(8,128)(2,1)}, u32[]{:S(2)}, u32[]{:S(2)}) collective-permute-start(bf16[256,2048]{1,0:T(8,128)(2,1)} %get-tuple-element.136), channel_id=1, source_target_pairs={{0,1},{2,3},{1,0},{3,2},{4,5},{6,7},{5,4},{7,6},{8,9},{10,11},{9,8... | collective-permute-start | bytes 3145736 | tf_op jit(solution)/shard_map/ppermute | solution.py:349
  60.0 25.2 %collective-permute-start.10 = (bf16[256,2048]{1,0:T(8,128)(2,1)S(1)}, bf16[256,2048]{1,0:T(8,128)(2,1)}, u32[]{:S(2)}, u32[]{:S(2)}) collective-permute-start(bf16[256,2048]{1,0:T(8,128)(2,1)S(1)} %copy-done.1), channel_id=1, source_target_pairs={{0,16},{4,20},{8,24},{12,28},{16,0},{20,4},{24,8},{28,12},{1,17},{... | collective-permute-start | bytes 3145736 | tf_op jit(solution)/shard_map/ppermute | solution.py:261
  61.5 11.9 %collective-permute-start.9 = (bf16[256,1024]{1,0:T(8,128)(2,1)}, bf16[256,1024]{1,0:T(8,128)(2,1)}, u32[]{:S(2)}, u32[]{:S(2)}) collective-permute-start(bf16[256,1024]{1,0:T(8,128)(2,1)} %get-tuple-element.140), channel_id=1, source_target_pairs={{1,2},{2,1},{5,6},{6,5},{9,10},{10,9},{13,14},{14,13},{17,18},{18,... | collective-permute-start | bytes 1572872 | tf_op jit(solution)/shard_map/ppermute | solution.py:349
  63.0 10.3 %collective-permute-start.8 = (f32[1,128]{1,0:T(1,128)S(1)}, f32[1,128]{1,0:T(1,128)S(1)}, u32[]{:S(2)}, u32[]{:S(2)}) collective-permute-start(f32[1,128]{1,0:T(1,128)S(1)} %add_rsqrt_fusion), channel_id=1, source_target_pairs={{0,4},{4,0},{8,12},{12,8},{16,20},{20,16},{24,28},{28,24},{1,5},{5... | collective-permute-start | bytes 1544 | tf_op jit(solution)/shard_map/ppermute | solution.py:261
  73.4 34.8 %copy-start.21 = (f32[256,1]{1,0:T(8,128)}, f32[256,1]{1,0:T(8,128)S(1)}, u32[]{:S(2)}) copy-start(f32[256,1]{1,0:T(8,128)S(1)} %copy.6.refs_2_) | copy-start | bytes 3076
  85.2 15.1 %copy-start.41 = (bf16[256,2048]{1,0:T(8,128)(2,1)}, bf16[256,2048]{1,0:T(8,128)(2,1)S(1)}, u32[]{:S(2)}) copy-start(bf16[256,2048]{1,0:T(8,128)(2,1)S(1)} %get-tuple-element.144.refs_0_) | copy-start | bytes 3145732
  85.2 23.0 %copy-start.15 = (bf16[256,2048]{1,0:T(8,128)(2,1)S(1)}, bf16[256,2048]{1,0:T(8,128)(2,1)}, u32[]{:S(2)}) copy-start(bf16[256,2048]{1,0:T(8,128)(2,1)} %get-tuple-element.147.refs_4_.refs_0_) | copy-start | bytes 3145732
  85.2 23.0 %collective-permute-start.11 = (bf16[256,2048]{1,0:T(8,128)(2,1)S(1)}, bf16[256,2048]{1,0:T(8,128)(2,1)S(1)}, u32[]{:S(2)}, u32[]{:S(2)}) collective-permute-start(bf16[256,2048]{1,0:T(8,128)(2,1)S(1)} %get-tuple-element.144.refs_0_), channel_id=1, source_target_pairs={{0,1},{2,3},{1,0},{3,2},{4,5},{6,7},{5,4},{7,6},{8,9},{10,11},{9,8... | collective-permute-start | bytes 3145736 | tf_op jit(solution)/shard_map/ppermute | solution.py:349
  86.7 21.5 %collective-permute-start.12 = (bf16[256,2048]{1,0:T(8,128)(2,1)S(1)}, bf16[256,2048]{1,0:T(8,128)(2,1)S(1)}, u32[]{:S(2)}, u32[]{:S(2)}) collective-permute-start(bf16[256,2048]{1,0:T(8,128)(2,1)S(1)} %get-tuple-element.148), channel_id=1, source_target_pairs={{1,2},{2,1},{5,6},{6,5},{9,10},{10,9},{13,14},{14,13},{17,18},{18,... | collective-permute-start | bytes 3145736 | tf_op jit(solution)/shard_map/ppermute | solution.py:349
  111.1 36.5 %collective-permute-start.13 = (bf16[256,2560]{1,0:T(8,128)(2,1)}, bf16[256,2560]{1,0:T(8,128)(2,1)S(1)}, u32[]{:S(2)}, u32[]{:S(2)}) collective-permute-start(bf16[256,2560]{1,0:T(8,128)(2,1)} %get-tuple-element.155.refs_4_), channel_id=1, source_target_pairs={{0,1},{2,3},{1,0},{3,2},{4,5},{6,7},{5,4},{7,6},{8,9},{10,11},{9,8... | collective-permute-start | bytes 3932168 | tf_op jit(solution)/shard_map/ppermute | solution.py:349
  114.6 33.0 %collective-permute-start.15 = (bf16[256,2048]{1,0:T(8,128)(2,1)}, bf16[256,2048]{1,0:T(8,128)(2,1)S(1)}, u32[]{:S(2)}, u32[]{:S(2)}) collective-permute-start(bf16[256,2048]{1,0:T(8,128)(2,1)} %get-tuple-element.158), channel_id=1, source_target_pairs={{1,2},{2,1},{5,6},{6,5},{9,10},{10,9},{13,14},{14,13},{17,18},{18,... | collective-permute-start | bytes 3145736 | tf_op jit(solution)/shard_map/ppermute | solution.py:349
  115.3 33.9 %collective-permute-start.16 = (bf16[256,2048]{1,0:T(8,128)(2,1)S(1)}, bf16[256,2048]{1,0:T(8,128)(2,1)}, u32[]{:S(2)}, u32[]{:S(2)}) collective-permute-start(bf16[256,2048]{1,0:T(8,128)(2,1)S(1)} %copy-done.1), channel_id=1, source_target_pairs={{0,24},{4,28},{8,16},{12,20},{16,8},{20,12},{24,0},{28,4},{1,25},{... | collective-permute-start | bytes 3145736 | tf_op jit(solution)/shard_map/ppermute | solution.py:261
  117.8 20.0 %collective-permute-start.14 = (f32[2,128]{1,0:T(2,128)S(1)}, f32[2,128]{1,0:T(2,128)S(1)}, u32[]{:S(2)}, u32[]{:S(2)}) collective-permute-start(f32[2,128]{1,0:T(2,128)S(1)} %pad_maximum_fusion.1), channel_id=1, source_target_pairs={{0,8},{4,12},{8,0},{12,4},{16,24},{20,28},{24,16},{28,20},{1,9},{5... | collective-permute-start | bytes 3080 | tf_op jit(solution)/shard_map/ppermute | solution.py:261
  149.2 16.4 %copy-start.36 = (bf16[256,2560]{1,0:T(8,128)(2,1)}, bf16[256,2560]{1,0:T(8,128)(2,1)S(1)}, u32[]{:S(2)}) copy-start(bf16[256,2560]{1,0:T(8,128)(2,1)S(1)} %get-tuple-element.162.refs_0_) | copy-start | bytes 3932164
  149.2 27.4 %copy-start.17 = (bf16[256,2048]{1,0:T(8,128)(2,1)S(1)}, bf16[256,2048]{1,0:T(8,128)(2,1)}, u32[]{:S(2)}) copy-start(bf16[256,2048]{1,0:T(8,128)(2,1)} %get-tuple-element.153.refs_5_.refs_0_) | copy-start | bytes 3145732
  149.2 27.4 %collective-permute-start.17 = (bf16[256,2560]{1,0:T(8,128)(2,1)S(1)}, bf16[256,2560]{1,0:T(8,128)(2,1)S(1)}, u32[]{:S(2)}, u32[]{:S(2)}) collective-permute-start(bf16[256,2560]{1,0:T(8,128)(2,1)S(1)} %get-tuple-element.162.refs_0_), channel_id=1, source_target_pairs={{0,1},{2,3},{1,0},{3,2},{4,5},{6,7},{5,4},{7,6},{8,9},{10,11},{9,8... | collective-permute-start | bytes 3932168 | tf_op jit(solution)/shard_map/ppermute | solution.py:349
  152.0 24.6 %collective-permute-start.18 = (bf16[256,2560]{1,0:T(8,128)(2,1)S(1)}, bf16[256,2560]{1,0:T(8,128)(2,1)S(1)}, u32[]{:S(2)}, u32[]{:S(2)}) collective-permute-start(bf16[256,2560]{1,0:T(8,128)(2,1)S(1)} %get-tuple-element.165), channel_id=1, source_target_pairs={{1,2},{2,1},{5,6},{6,5},{9,10},{10,9},{13,14},{14,13},{17,18},{18,... | collective-permute-start | bytes 3932168 | tf_op jit(solution)/shard_map/ppermute | solution.py:349
  179.6 30.4 %collective-permute-start.19 = (bf16[256,2816]{1,0:T(8,128)(2,1)}, bf16[256,2816]{1,0:T(8,128)(2,1)S(1)}, u32[]{:S(2)}, u32[]{:S(2)}) collective-permute-start(bf16[256,2816]{1,0:T(8,128)(2,1)} %get-tuple-element.168.refs_4_), channel_id=1, source_target_pairs={{0,1},{2,3},{1,0},{3,2},{4,5},{6,7},{5,4},{7,6},{8,9},{10,11},{9,8... | collective-permute-start | bytes 4325384 | tf_op jit(solution)/shard_map/ppermute | solution.py:349
  183.2 15.6 %collective-permute-start.21 = (bf16[256,2560]{1,0:T(8,128)(2,1)}, bf16[256,2560]{1,0:T(8,128)(2,1)}, u32[]{:S(2)}, u32[]{:S(2)}) collective-permute-start(bf16[256,2560]{1,0:T(8,128)(2,1)} %get-tuple-element.171), channel_id=1, source_target_pairs={{1,2},{2,1},{5,6},{6,5},{9,10},{10,9},{13,14},{14,13},{17,18},{18,... | collective-permute-start | bytes 3932168 | tf_op jit(solution)/shard_map/ppermute | solution.py:349
  184.9 3.6 collective-permute-start.20
  189.2 20.7 %copy-start.27 = (bf16[256,1536]{1,0:T(8,128)(2,1)S(1)}, bf16[256,1536]{1,0:T(8,128)(2,1)}, u32[]{:S(2)}) copy-start(bf16[256,1536]{1,0:T(8,128)(2,1)} %copy-done.26) | copy-start | bytes 2359300
  189.2 20.7 %copy-start.40 = (f32[256,1]{1,0:T(8,128)S(1)}, f32[256,1]{1,0:T(8,128)}, u32[]{:S(2)}) copy-start(f32[256,1]{1,0:T(8,128)} %copy.10.refs_2_) | copy-start | bytes 3076
  198.7 15.1 %copy-start.28 = (bf16[256,1536]{1,0:T(8,128)(2,1)}, bf16[256,1536]{1,0:T(8,128)(2,1)S(1)}, u32[]{:S(2)}) copy-start(bf16[256,1536]{1,0:T(8,128)(2,1)S(1)} %get-tuple-element.190.refs_5_.refs_0_) | copy-start | bytes 2359300
  213.8 26.7 %collective-permute-start.23 = (bf16[256,2816]{1,0:T(8,128)(2,1)}, bf16[256,2816]{1,0:T(8,128)(2,1)S(1)}, u32[]{:S(2)}, u32[]{:S(2)}) collective-permute-start(bf16[256,2816]{1,0:T(8,128)(2,1)} %get-tuple-element.177), channel_id=1, source_target_pairs={{1,2},{2,1},{5,6},{6,5},{9,10},{10,9},{13,14},{14,13},{17,18},{18,... | collective-permute-start | bytes 4325384 | tf_op jit(solution)/shard_map/ppermute | solution.py:349
  214.7 25.8 %collective-permute-start.22 = (bf16[256,2560]{1,0:T(8,128)(2,1)S(1)}, bf16[256,2560]{1,0:T(8,128)(2,1)S(1)}, u32[]{:S(2)}, u32[]{:S(2)}) collective-permute-start(bf16[256,2560]{1,0:T(8,128)(2,1)S(1)} %get-tuple-element.174.refs_0_), channel_id=1, source_target_pairs={{0,1},{2,3},{1,0},{3,2},{4,5},{6,7},{5,4},{7,6},{8,9},{10,11},{9,8... | collective-permute-start | bytes 3932168 | tf_op jit(solution)/shard_map/ppermute | solution.py:349
  225.3 15.2 %copy-start.34 = (bf16[256,1024]{1,0:T(8,128)(2,1)}, bf16[256,1024]{1,0:T(8,128)(2,1)S(1)}, u32[]{:S(2)}) copy-start(bf16[256,1024]{1,0:T(8,128)(2,1)S(1)} %get-tuple-element.176.refs_3_.refs_6_) | copy-start | bytes 1572868
  225.3 15.2 %copy-start.20 = (bf16[256,2048]{1,0:T(8,128)(2,1)S(1)}, bf16[256,2048]{1,0:T(8,128)(2,1)}, u32[]{:S(2)}) copy-start(bf16[256,2048]{1,0:T(8,128)(2,1)} %get-tuple-element.178.refs_5_.refs_0_) | copy-start | bytes 3145732
  240.5 14.2 %copy-start.2 = (bf16[256,2048]{1,0:T(8,128)(2,1)S(1)}, bf16[256,2048]{1,0:T(8,128)(2,1)}, u32[]{:S(2)}) copy-start(bf16[256,2048]{1,0:T(8,128)(2,1)} %pad_maximum_fusion.x_ref) | copy-start | bytes 3145732
  243.4 31.5 %collective-permute-start.24 = (bf16[256,2816]{1,0:T(8,128)(2,1)}, bf16[256,2816]{1,0:T(8,128)(2,1)S(1)}, u32[]{:S(2)}, u32[]{:S(2)}) collective-permute-start(bf16[256,2816]{1,0:T(8,128)(2,1)} %get-tuple-element.191.refs_4_), channel_id=1, source_target_pairs={{0,1},{2,3},{1,0},{3,2},{4,5},{6,7},{5,4},{7,6},{8,9},{10,11},{9,8... | collective-permute-start | bytes 4325384 | tf_op jit(solution)/shard_map/ppermute | solution.py:349
  247.7 10.7 %collective-permute-start.26 = (bf16[256,2560]{1,0:T(8,128)(2,1)}, bf16[256,2560]{1,0:T(8,128)(2,1)}, u32[]{:S(2)}, u32[]{:S(2)}) collective-permute-start(bf16[256,2560]{1,0:T(8,128)(2,1)} %get-tuple-element.193), channel_id=1, source_target_pairs={{1,2},{2,1},{5,6},{6,5},{9,10},{10,9},{13,14},{14,13},{17,18},{18,... | collective-permute-start | bytes 3932168 | tf_op jit(solution)/shard_map/ppermute | solution.py:349
  249.5 4.5 %collective-permute-start.25 = (f32[2,128]{1,0:T(2,128)S(1)}, f32[2,128]{1,0:T(2,128)S(1)}, u32[]{:S(2)}, u32[]{:S(2)}) collective-permute-start(f32[2,128]{1,0:T(2,128)S(1)} %pad_maximum_fusion.1), channel_id=1, source_target_pairs={{0,24},{4,28},{8,16},{12,20},{16,8},{20,12},{24,0},{28,4},{1,25},{... | collective-permute-start | bytes 3080 | tf_op jit(solution)/shard_map/ppermute | solution.py:261
  254.7 20.1 %copy-start.29 = (bf16[256,1536]{1,0:T(8,128)(2,1)S(1)}, bf16[256,1536]{1,0:T(8,128)(2,1)}, u32[]{:S(2)}) copy-start(bf16[256,1536]{1,0:T(8,128)(2,1)} %copy-done.28) | copy-start | bytes 2359300
  254.7 20.1 %copy-start.35 = (bf16[256,1024]{1,0:T(8,128)(2,1)S(1)}, bf16[256,1024]{1,0:T(8,128)(2,1)}, u32[]{:S(2)}) copy-start(bf16[256,1024]{1,0:T(8,128)(2,1)} %copy-done.34) | copy-start | bytes 1572868
  254.7 20.1 %copy-start.39 = (f32[256,1]{1,0:T(8,128)S(1)}, f32[256,1]{1,0:T(8,128)}, u32[]{:S(2)}) copy-start(f32[256,1]{1,0:T(8,128)} %copy.12.refs_2_) | copy-start | bytes 3076
  274.9 30.3 %copy-start.33 = (bf16[256,1024]{1,0:T(8,128)(2,1)S(1)}, bf16[256,1024]{1,0:T(8,128)(2,1)}, u32[]{:S(2)}) copy-start(bf16[256,1024]{1,0:T(8,128)(2,1)} %copy-done.32) | copy-start | bytes 1572868
  277.6 28.9 %copy-start.38 = (bf16[256,2560]{1,0:T(8,128)(2,1)}, bf16[256,2560]{1,0:T(8,128)(2,1)S(1)}, u32[]{:S(2)}) copy-start(bf16[256,2560]{1,0:T(8,128)(2,1)S(1)} %get-tuple-element.196.refs_0_) | copy-start | bytes 3932164
  277.6 27.6 %collective-permute-start.27 = (bf16[256,2560]{1,0:T(8,128)(2,1)S(1)}, bf16[256,2560]{1,0:T(8,128)(2,1)S(1)}, u32[]{:S(2)}, u32[]{:S(2)}) collective-permute-start(bf16[256,2560]{1,0:T(8,128)(2,1)S(1)} %get-tuple-element.196.refs_0_), channel_id=1, source_target_pairs={{0,1},{2,3},{1,0},{3,2},{4,5},{6,7},{5,4},{7,6},{8,9},{10,11},{9,8... | collective-permute-start | bytes 3932168 | tf_op jit(solution)/shard_map/ppermute | solution.py:349
  279.6 0.7 collective-permute-start.28
  305.2 20.6 %copy-start.22 = (f32[256,1]{1,0:T(8,128)S(1)}, f32[256,1]{1,0:T(8,128)}, u32[]{:S(2)}) copy-start(f32[256,1]{1,0:T(8,128)} %copy-done.21) | copy-start | bytes 3076
  306.5 38.0 %copy-start.43 = (bf16[256,1792]{1,0:T(8,128)(2,1)}, bf16[256,1792]{1,0:T(8,128)(2,1)S(1)}, u32[]{:S(2)}) copy-start(bf16[256,1792]{1,0:T(8,128)(2,1)S(1)} %get-tuple-element.198.refs_4_) | copy-start | bytes 2752516
  306.5 19.3 %collective-permute-start.29 = (bf16[256,1792]{1,0:T(8,128)(2,1)S(1)}, bf16[256,1792]{1,0:T(8,128)(2,1)S(1)}, u32[]{:S(2)}, u32[]{:S(2)}) collective-permute-start(bf16[256,1792]{1,0:T(8,128)(2,1)S(1)} %get-tuple-element.198.refs_4_), channel_id=1, source_target_pairs={{0,1},{2,3},{1,0},{3,2},{4,5},{6,7},{5,4},{7,6},{8,9},{10,11},{9,8... | collective-permute-start | bytes 2752520 | tf_op jit(solution)/shard_map/ppermute | solution.py:349
  308.5 0.7 collective-permute-start.30
  309.2 35.3 %copy-start.23 = (bf16[256,1536]{1,0:T(8,128)(2,1)}, bf16[256,1536]{1,0:T(8,128)(2,1)S(1)}, u32[]{:S(2)}) copy-start(bf16[256,1536]{1,0:T(8,128)(2,1)S(1)} %collective-permute-done.30.refs_3_) | copy-start | bytes 2359300
  325.8 36.3 %copy-start.8 = (bf16[256,1792]{1,0:T(8,128)(2,1)}, bf16[256,1792]{1,0:T(8,128)(2,1)S(1)}, u32[]{:S(2)}) copy-start(bf16[256,1792]{1,0:T(8,128)(2,1)S(1)} %collective-permute-done.29.refs_1_.refs_6_.refs_5_) | copy-start | bytes 2752516
  327.1 16.3 %collective-permute-start.31 = (bf16[256,1536]{1,0:T(8,128)(2,1)S(1)}, bf16[256,1536]{1,0:T(8,128)(2,1)S(1)}, u32[]{:S(2)}, u32[]{:S(2)}) collective-permute-start(bf16[256,1536]{1,0:T(8,128)(2,1)S(1)} %get-tuple-element.202.refs_0_), channel_id=1, source_target_pairs={{0,1},{2,3},{1,0},{3,2},{4,5},{6,7},{5,4},{7,6},{8,9},{10,11},{9,8... | collective-permute-start | bytes 2359304 | tf_op jit(solution)/shard_map/ppermute | solution.py:349
  329.0 0.7 collective-permute-start.32
  343.3 34.8 %copy-start.9 = (bf16[256,1536]{1,0:T(8,128)(2,1)}, bf16[256,1536]{1,0:T(8,128)(2,1)S(1)}, u32[]{:S(2)}) copy-start(bf16[256,1536]{1,0:T(8,128)(2,1)S(1)} %collective-permute-done.31.refs_1_.refs_2_) | copy-start | bytes 2359300
  344.6 33.0 %collective-permute-start.33 = (bf16[256,768]{1,0:T(8,128)(2,1)S(1)}, bf16[256,768]{1,0:T(8,128)(2,1)S(1)}, u32[]{:S(2)}, u32[]{:S(2)}) collective-permute-start(bf16[256,768]{1,0:T(8,128)(2,1)S(1)} %get-tuple-element.204.refs_0_), channel_id=1, source_target_pairs={{0,1},{2,3},{1,0},{3,2},{4,5},{6,7},{5,4},{7,6},{8,9},{10,11},{9,8... | collective-permute-start | bytes 1179656 | tf_op jit(solution)/shard_map/ppermute | solution.py:349
  359.9 57.1 %collective-permute-start.38 = (bf16[256,2048]{1,0:T(8,128)(2,1)S(1)}, bf16[256,2048]{1,0:T(8,128)(2,1)S(1)}, u32[]{:S(2)}, u32[]{:S(2)}) collective-permute-start(bf16[256,2048]{1,0:T(8,128)(2,1)S(1)} %shard_map.82), channel_id=1, source_target_pairs={{0,8},{4,12},{8,0},{12,4},{16,24},{20,28},{24,16},{28,20},{1,9},{5... | collective-permute-start | bytes 3145736 | tf_op jit(solution)/shard_map/ppermute | solution.py:261
  361.4 16.1 %collective-permute-start.34 = (bf16[256,512]{1,0:T(8,128)(2,1)S(1)}, bf16[256,512]{1,0:T(8,128)(2,1)S(1)}, u32[]{:S(2)}, u32[]{:S(2)}) collective-permute-start(bf16[256,512]{1,0:T(8,128)(2,1)S(1)} %get-tuple-element.205), channel_id=1, source_target_pairs={{1,2},{2,1},{5,6},{6,5},{9,10},{10,9},{13,14},{14,13},{17,18},{18,... | collective-permute-start | bytes 786440 | tf_op jit(solution)/shard_map/ppermute | solution.py:349
  377.0 40.0 %collective-permute-start.39 = (bf16[256,2048]{1,0:T(8,128)(2,1)}, bf16[256,2048]{1,0:T(8,128)(2,1)S(1)}, u32[]{:S(2)}, u32[]{:S(2)}) collective-permute-start(bf16[256,2048]{1,0:T(8,128)(2,1)} %shard_map.83), channel_id=1, source_target_pairs={{0,16},{4,20},{8,24},{12,28},{16,0},{20,4},{24,8},{28,12},{1,17},{... | collective-permute-start | bytes 3145736 | tf_op jit(solution)/shard_map/ppermute | solution.py:261
  393.2 23.9 %collective-permute-start.40 = (bf16[256,2048]{1,0:T(8,128)(2,1)}, bf16[256,2048]{1,0:T(8,128)(2,1)S(1)}, u32[]{:S(2)}, u32[]{:S(2)}) collective-permute-start(bf16[256,2048]{1,0:T(8,128)(2,1)} %shard_map.84), channel_id=1, source_target_pairs={{0,24},{4,28},{8,16},{12,20},{16,8},{20,12},{24,0},{28,4},{1,25},{... | collective-permute-start | bytes 3145736 | tf_op jit(solution)/shard_map/ppermute | solution.py:261
  394.7 6.7 %collective-permute-start.36 = (bf16[256,512]{1,0:T(8,128)(2,1)S(1)}, bf16[256,512]{1,0:T(8,128)(2,1)S(1)}, u32[]{:S(2)}, u32[]{:S(2)}) collective-permute-start(bf16[256,512]{1,0:T(8,128)(2,1)S(1)} %get-tuple-element.209), channel_id=1, source_target_pairs={{0,1},{2,3},{1,0},{3,2},{4,5},{6,7},{5,4},{7,6},{8,9},{10,11},{9,8... | collective-permute-start | bytes 786440 | tf_op jit(solution)/shard_map/ppermute | solution.py:349
  397.0 0.7 collective-permute-start.35
  401.4 10.3 %collective-permute-start.37 = (bf16[256,256]{1,0:T(8,128)(2,1)S(1)}, bf16[256,256]{1,0:T(8,128)(2,1)S(1)}, u32[]{:S(2)}, u32[]{:S(2)}) collective-permute-start(bf16[256,256]{1,0:T(8,128)(2,1)S(1)} %shard_map.79), channel_id=1, source_target_pairs={{0,1},{2,3},{1,0},{3,2},{4,5},{6,7},{5,4},{7,6},{8,9},{10,11},{9,8... | collective-permute-start | bytes 393224 | tf_op jit(solution)/shard_map/ppermute | solution.py:349
  419.3 2.0 collective-permute-start.41
  (23 other events, 107.7 us)

commit v2 on v1

--- a/solution.py
+++ b/solution.py
@@ -14,6 +14,7 @@
 LAST = (2, 1)
 AHEAD = 3
 ROW_TILE = 32
+DOWN_TILE = 512
 KERNEL_VMEM = 52 * 2**20
 SMALL_VMEM = 8 * 2**20
 
@@ -25,25 +26,37 @@
 
 
 def gate_up_kernel(blocks, start, unit, off_ref, x_ref, gate_hbm, up_hbm, far_ref, near_ref):
+    wide = 2 if blocks % 2 == 0 else 1
+    per_flow = blocks // wide
+
     def step(gate_ref, up_ref):
         i = pl.program_id(0)
         x = x_ref[...]
         gate = jnp.dot(x, gate_ref[...], preferred_element_type=jnp.float32).astype(jnp.bfloat16)
         up = jnp.dot(x, up_ref[...], preferred_element_type=jnp.float32).astype(jnp.bfloat16)
 
-        def write(ref, u):
-            at = pl.multiple_of(2 * unit * u, 2 * unit)
-            ref[:, pl.ds(at, unit)] = gate
-            ref[:, pl.ds(at + unit, unit)] = up
-
-        pl.when(i < blocks)(lambda: write(far_ref, i))
-        pl.when(i >= blocks)(lambda: write(near_ref, i - blocks))
-
-    def weight_at(i):
-        return 0, off_ref[i // blocks] + start + i - (i // blocks) * blocks
-
-    weight = pl.BlockSpec((x_ref.shape[1], unit), weight_at)
-    pltpu.emit_pipeline(step, grid=(2 * blocks,), in_specs=[weight, weight])(gate_hbm, up_hbm)
+        def write(ref, block):
+            for w in range(wide):
+                at = pl.multiple_of(2 * unit * (wide * block + w), 2 * unit)
+                ref[:, pl.ds(at, unit)] = gate[:, w * unit : (w + 1) * unit]
+                ref[:, pl.ds(at + unit, unit)] = up[:, w * unit : (w + 1) * unit]
+
+        pl.when(i < per_flow)(lambda: write(far_ref, i))
+        pl.when(i >= per_flow)(lambda: write(near_ref, i - per_flow))
+
+    depth = x_ref.shape[1]
+    if wide == 1:
+        weight = pl.BlockSpec(
+            (depth, unit), lambda i: (0, off_ref[i // blocks] + start + i - (i // blocks) * blocks)
+        )
+        pltpu.emit_pipeline(step, grid=(2 * blocks,), in_specs=[weight, weight])(gate_hbm, up_hbm)
+        return
+    weight = pl.BlockSpec(
+        (pl.Element(depth), pl.Element(wide * unit)),
+        lambda i: (0, pl.multiple_of(
+            (off_ref[i // per_flow] + start + wide * (i - (i // per_flow) * per_flow)) * unit, unit)),
+    )
+    pltpu.emit_pipeline(step, grid=(2 * per_flow,), in_specs=[weight, weight])(gate_hbm, up_hbm)
 
 
 def gate_up(x, gate_weight, up_weight, offsets, start, blocks, unit):
@@ -63,68 +76,56 @@
     )(offsets, x, gate_weight, up_weight)
 
 
-def down_kernel(steps, starts, places, unit, n_roles, has_total, off_ref, weight_hbm, *refs):
-    out_ref, acc_ref = refs[-2:]
-    rows, width = out_ref.shape
-    count = sum(size for _, _, _, size in steps)
-    acc_ref[...] = refs[-3][...] if has_total else jnp.zeros_like(acc_ref)
-
-    def weight_at(k):
-        index = 0
-        for flow, chunk, first, size in steps:
-            index = jnp.where(k >= first, off_ref[1 - flow] + starts[chunk] + k - first, index)
-        return index, 0
+def down_kernel(parts, unit, tile, n_roles, has_total, off_ref, weight_hbm, *refs):
+    out_hbm = refs[-1]
+    rows, width = out_hbm.shape
+    column = pl.BlockSpec((rows, tile), lambda j: (0, j))
 
     def run(role):
-        def step(weight_ref, *pieces):
-            k = pl.program_id(0)
-            for (flow, chunk, first, size), ref in zip(steps, pieces):
-                @pl.when((k >= first) & (k < first + size))
-                def _():
-                    acc_ref[...] += jnp.dot(ref[...], weight_ref[...], preferred_element_type=jnp.float32)
-
-        specs, operands = [pl.BlockSpec((unit, width), weight_at)], [weight_hbm]
-        for flow, chunk, first, size in steps:
-            index = (2 * chunk + flow) * n_roles + role
-            at = places[index]
-            specs.append(pl.BlockSpec(
-                (rows, unit),
-                lambda k, at=at, first=first, size=size: (0, at + jnp.clip(k - first, 0, size - 1)),
-            ))
-            operands.append(refs[index])
-        pltpu.emit_pipeline(step, grid=(count,), in_specs=specs)(*operands)
+        weights, hidden, specs = [], [], []
+        for p, (flow, start, size, places) in enumerate(parts):
+            first = pl.multiple_of((off_ref[1 - flow] + start) * unit, unit)
+            weights.append(weight_hbm.at[pl.ds(first, size * unit), :])
+            hidden.append(refs[p * n_roles + role].at[:, pl.ds(places[role] * unit, size * unit)])
+            specs.append(pl.BlockSpec((size * unit, tile), lambda j: (0, j)))
+        specs += [pl.BlockSpec((rows, size * unit), lambda j: (0, 0)) for _, _, size, _ in parts]
+        extra = [refs[-2]] if has_total else []
+
+        def step(*blocks):
+            total = blocks[2 * len(parts)][...] if has_total else None
+            for weight, value in zip(blocks[: len(parts)], blocks[len(parts) :]):
+                part = jnp.dot(value[...], weight[...], preferred_element_type=jnp.float32)
+                total = part if total is None else total + part
+            blocks[-1][...] = total.astype(blocks[-1].dtype)
+
+        pltpu.emit_pipeline(
+            step, grid=(width // tile,), in_specs=specs + [column for _ in extra], out_specs=[column]
+        )(*weights, *hidden, *extra, out_hbm)
 
     for role in range(n_roles):
         pl.when(off_ref[2] == role)(functools.partial(run, role))
-    out_ref[...] = acc_ref[...].astype(out_ref.dtype)
 
 
 def down(group, weight, offsets, unit, total, dtype):
     n_roles = len(group[0][2])
     rows, width = group[0][2][0][0].shape[0], weight.shape[1]
-    steps, at = [], 0
-    for flow in range(2):
-        for chunk, (_, size, _, _) in enumerate(group):
-            steps.append((flow, chunk, at, size))
-            at += size
-    pieces = [piece for chunk in group for flow in range(2) for piece in chunk[2 + flow]]
-    starts = [chunk[0] for chunk in group]
+    parts, pieces = [], []
+    for start, size, *flows in group:
+        for flow, by_role in enumerate(flows):
+            parts.append((flow, start, size, [place for _, place in by_role]))
+            pieces += [message for message, _ in by_role]
+    depth = unit * sum(size for _, _, size, _ in parts)
     extra = () if total is None else (total,)
     return pl.pallas_call(
-        functools.partial(
-            down_kernel, steps, starts, [place for _, place in pieces], unit, n_roles, total is not None
-        ),
-        in_specs=[SMEM, HBM] + [ANY] * len(pieces) + [VMEM for _ in extra],
-        out_specs=VMEM,
-        scratch_shapes=[pltpu.VMEM((rows, width), jnp.float32)],
+        functools.partial(down_kernel, parts, unit, min(DOWN_TILE, width), n_roles, total is not None),
+        in_specs=[SMEM, HBM] + [ANY] * (len(pieces) + len(extra)),
+        out_specs=ANY,
         out_shape=jax.ShapeDtypeStruct((rows, width), dtype),
         compiler_params=pltpu.CompilerParams(vmem_limit_bytes=KERNEL_VMEM),
         cost_estimate=pl.CostEstimate(
-            flops=2 * rows * width * at * unit,
-            bytes_accessed=2 * width * at * unit,
-            transcendentals=0,
+            flops=2 * rows * width * depth, bytes_accessed=2 * width * depth, transcendentals=0
         ),
-    )(offsets, weight, *[message for message, _ in pieces], *extra)
+    )(offsets, weight, *pieces, *extra)
 
 
 def exchange_kernel(jobs, unit, n_in, role_ref, *refs):
@@ -245,9 +246,9 @@
     groups, due = {}, {}
     for i, (pair, _, _) in enumerate(chunks):
         arrival = when[i][-1]
-        if pair:
+        if 0 < pair < n_pair - 1:
             arrival = max(when[j][-1] for j in range(count) if chunks[j][0] == pair)
-        elif i < count // 2:
+        elif pair == 0 and i < count // 2:
             arrival = max(when[j][-1] for j in range(count // 2) if chunks[j][0] == pair)
         groups.setdefault((arrival, pair), []).append(i)
     for arrival, pair in groups:
@@ -275,7 +276,13 @@
 
     col_masks = [1 << b for b in range(n_col.bit_length() - 1)]
     far, near, came, sent, totals, outs = {}, {}, {}, {}, {}, {}
+    if n_pair > 1:
+        lhs[1] = along_row(lhs[0], 2)
+    squares = squares + along_col(squares, col_masks[0])
     far[0], near[0] = start_chunk(0, lhs[0])
+    stages = {t: mask for t, mask in enumerate(col_masks[1:])}
+    ready = max(2, len(col_masks) - 1)
+    stages[ready], stages[ready + 1] = "core", "row"
     carried = {}
     for t in range(last_step + 1):
         jobs, widths, sides, operands, known = [], [], [], [], {}
@@ -325,12 +332,11 @@
             messages.update(zip(sides, exchange(jobs, widths, operands, offsets, unit)))
 
         extra = {}
-        wanted = [pair for pair in range(1, n_pair) if max(0, first_use[pair] - AHEAD) == t]
+        wanted = [pair for pair in range(2, n_pair) if max(0, first_use[pair] - AHEAD) == t]
         if wanted:
             extra["gained"] = lhs[0]
-        if t + 1 < count:
-            extra["x"] = lhs[chunks[t + 1][0]]
-        if t <= len(col_masks) + 1:
+        stage = stages.get(t)
+        if stage:
             extra["squares"] = squares
         arrived = [(pair, members) for (arrival, pair), members in groups.items() if arrival == t]
         for pair, members in arrived:
@@ -350,16 +356,16 @@
             sent[t, side] = value
         for pair in wanted:
             lhs[pair] = along_row(extra["gained"], 2 * pair)
-        if t < len(col_masks):
-            squares = extra["squares"] + along_col(extra["squares"], col_masks[t])
-        elif t == len(col_masks):
+        if stage == "core":
             scale = lax.rsqrt(extra["squares"] / (depth * n_col) + 1e-05)
             squares = scales[0] = jnp.concatenate([scale, along_row(scale, 1)], axis=0)
-        elif t == len(col_masks) + 1:
+        elif stage == "row":
             for pair in range(1, n_pair):
                 scales[pair] = along_row(extra["squares"], 2 * pair)
-        if "x" in extra:
-            far[t + 1], near[t + 1] = start_chunk(t + 1, extra["x"])
+        elif stage:
+            squares = extra["squares"] + along_col(extra["squares"], stage)
+        if t + 1 < count:
+            far[t + 1], near[t + 1] = start_chunk(t + 1, lhs[chunks[t + 1][0]])
         for pair, members in arrived:
             group = []
             for i in members:

time: 425 us -> 400 us (0.941)
  waiting for transfers between devices: 162 us -> 141 us
  Pallas kernels: 184 us -> 168 us
  local copies, waits for them, and re-layouts: 4.99 us -> 18.4 us
    ppermute x12, waiting for transfers between devices: 38.1 us -> 3.98 us  [along_row(): return lax.ppermute(value, 'row', [(r, r ^ mask) for r in range(n_row)])]
    unnamed x90 -> x106, local copies, waits for them, and re-layouts: 3.06 us -> 17.2 us
    ppermute x28, waiting for transfers between devices: 119 us -> 127 us  [body(): came[t, side] = lax.ppermute(value, 'col', side_pairs(side, n_col))]
    pallas_call x10, Pallas kernels: 91.4 us -> 83.8 us  [gate_up(): pl.pallas_call(functools.partial(gate_up_kernel, blocks, start, unit), in...]
    ppermute x2, waiting for transfers between devices: 4.87 us -> 10.5 us  [along_col(): return lax.ppermute(value, 'col', [(c, c ^ mask) for c in range(n_col)])]
    pallas_call x6 -> x7, Pallas kernels: 66.5 us -> 61.9 us  [down(): pl.pallas_call(functools.partial(down_kernel, parts, unit, min(DOWN_TILE,...]
  transfers between devices with their start and end apart: 42 -> 42, of which waited for: 17 -> 15; matrix products, arithmetic and copies ran while one was open for 0% -> 0% of each run, Pallas kernels for 37% -> 38%
where the time goes in v2:
time: 400 us; the launch traced here: 397 us
  Pallas kernels  168 us (42%)
  waiting for transfers between devices  141 us (35%)
  starting transfers between devices  64.5 us (16%)
  local copies, waits for them, and re-layouts  18.4 us (5%)
  other arithmetic  4.6 us (1%)
    ppermute x28, waiting for transfers between devices, body(): came[t, side] = lax.ppermute(value, 'col', side_pairs(side, n_col))  127 us
    pallas_call x10, Pallas kernels, gate_up(): pl.pallas_call(functools.partial(gate_up_kernel, blocks, start, unit), in...  83.8 us
    pallas_call x7, Pallas kernels, down(): pl.pallas_call(functools.partial(down_kernel, parts, unit, min(DOWN_TILE,...  61.9 us
    ppermute x28, starting transfers between devices, body(): came[t, side] = lax.ppermute(value, 'col', side_pairs(side, n_col))  48.8 us
    pallas_call x14, Pallas kernels, exchange(): pl.pallas_call(functools.partial(exchange_kernel, jobs, unit, len(operand...  22 us
    unnamed x106, local copies, waits for them, and re-layouts  17.2 us
    ppermute x12, starting transfers between devices, along_row(): return lax.ppermute(value, 'row', [(r, r ^ mask) for r in range(n_row)])  13.1 us
    ppermute x2, waiting for transfers between devices, along_col(): return lax.ppermute(value, 'col', [(c, c ^ mask) for c in range(n_col)])  10.5 us
  transfers between devices with their start and end apart: 42, of which 15 were waited for; matrix products, arithmetic and copies ran while one was open for 0% of the time, Pallas kernels for 38%

profile of v2, /device:TPU:0, one launch (start us, length us, event | category | flops | bytes accessed | tf_op | source)
XLA Modules:
  0.0 397.3 jit_solution(8373497132438342959)
XLA Ops:
  1.8 2.6 collective-permute-start.2
  4.6 1.7 collective-permute-start.1
  6.4 6.2 %shard_map.57 = (bf16[256,1024]{1,0:T(8,128)(2,1)S(1)}, bf16[256,1024]{1,0:T(8,128)(2,1)S(1)}) custom-call(s32[3]{0:T(128)S(1)} %pad_add_fusion.off_ref.role_ref, bf16[256,2048]{1,0:T(8,128)(2,1)} %copy-done, bf16[2048,3584]{1,0:T(8,128)(2,1)} %gate_hbm.19, bf16[2048,3584]{1,0:T(8,128)(2,1)} %up_hbm.19), custom_call_target="tpu_custom_call" | custom-call | flops 2147483648 | bytes 8388608 | tf_op jit(solution)/shard_map/pallas_call | solution.py:65
  12.6 1.7 collective-permute-start.3
  14.4 6.2 %shard_map.59 = (bf16[256,1024]{1,0:T(8,128)(2,1)S(1)}, bf16[256,1024]{1,0:T(8,128)(2,1)S(1)}) custom-call(s32[3]{0:T(128)S(1)} %pad_add_fusion.off_ref.role_ref, bf16[256,2048]{1,0:T(8,128)(2,1)} %copy-done, bf16[2048,3584]{1,0:T(8,128)(2,1)} %gate_hbm.19, bf16[2048,3584]{1,0:T(8,128)(2,1)} %up_hbm.19), custom_call_target="tpu_custom_call" | custom-call | flops 2147483648 | bytes 8388608 | tf_op jit(solution)/shard_map/pallas_call | solution.py:65
  20.6 5.8 %collective-permute-done.3.refs_2_ = bf16[256,1024]{1,0:T(8,128)(2,1)S(1)} collective-permute-done((bf16[256,1024]{1,0:T(8,128)(2,1)S(1)}, bf16[256,1024]{1,0:T(8,128)(2,1)S(1)}, u32[]{:S(2)}, u32[]{:S(2)}) %collective-permute-start.3) | collective-permute-done | bytes 524320 | tf_op jit(solution)/shard_map/ppermute | solution.py:355
  27.6 4.6 %collective-permute-start.5 = (bf16[256,1024]{1,0:T(8,128)(2,1)S(1)}, bf16[256,1024]{1,0:T(8,128)(2,1)S(1)}, u32[]{:S(2)}, u32[]{:S(2)}) collective-permute-start(bf16[256,1024]{1,0:T(8,128)(2,1)S(1)} %get-tuple-element.115.refs_0_.refs_3_), channel_id=1, source_target_pairs={{0,1},{2,3},{1,0},{3,2},{4,5},{6,7},{5,4},{7,6},{8,9},{10,11},{9,8... | collective-permute-start | bytes 1572872 | tf_op jit(solution)/shard_map/ppermute | solution.py:355
  32.2 10.5 %collective-permute-done.6 = f32[1,128]{1,0:T(1,128)S(1)} collective-permute-done((f32[1,128]{1,0:T(1,128)S(1)}, f32[1,128]{1,0:T(1,128)S(1)}, u32[]{:S(2)}, u32[]{:S(2)}) %collective-permute-start.6) | collective-permute-done | bytes 544 | tf_op jit(solution)/shard_map/ppermute | solution.py:265
  43.7 11.1 %shard_map.58 = (bf16[256,2048]{1,0:T(8,128)(2,1)S(1)}, bf16[256,2048]{1,0:T(8,128)(2,1)}) custom-call(s32[3]{0:T(128)S(1)} %pad_add_fusion.off_ref.role_ref, bf16[256,2048]{1,0:T(8,128)(2,1)} %copy-done.52, bf16[2048,3584]{1,0:T(8,128)(2,1)} %gate_hbm.19, bf16[2048,3584]{1,0:T(8,128)(2,1)} %up_hbm.19), custom_call_target="tpu_custom_call" | custom-call | flops 4294967296 | bytes 16777216 | tf_op jit(solution)/shard_map/pallas_call | solution.py:65
  54.8 1.8 shard_map.61
  56.6 2.0 collective-permute-start.7
  58.6 1.5 collective-permute-start.11
  60.2 1.4 collective-permute-start.9
  61.6 9.4 %shard_map.62 = (bf16[256,1536]{1,0:T(8,128)(2,1)S(1)}, bf16[256,1536]{1,0:T(8,128)(2,1)S(1)}) custom-call(s32[3]{0:T(128)S(1)} %pad_add_fusion.off_ref.role_ref, bf16[256,2048]{1,0:T(8,128)(2,1)} %copy-done.52, bf16[2048,3584]{1,0:T(8,128)(2,1)} %gate_hbm.19, bf16[2048,3584]{1,0:T(8,128)(2,1)} %up_hbm.19), custom_call_target="tpu_custom_call" | custom-call | flops 3221225472 | bytes 12582912 | tf_op jit(solution)/shard_map/pallas_call | solution.py:65
  72.1 7.7 %collective-permute-done.7.refs_1_ = bf16[256,2048]{1,0:T(8,128)(2,1)} collective-permute-done((bf16[256,2048]{1,0:T(8,128)(2,1)}, bf16[256,2048]{1,0:T(8,128)(2,1)}, u32[]{:S(2)}, u32[]{:S(2)}) %collective-permute-start.7) | collective-permute-done | bytes 1048608 | tf_op jit(solution)/shard_map/ppermute | solution.py:355
  80.8 2.1 shard_map.63
  82.9 1.5 collective-permute-start.12
  85.1 11.0 %shard_map.67 = (bf16[256,2048]{1,0:T(8,128)(2,1)S(1)}, bf16[256,2048]{1,0:T(8,128)(2,1)}) custom-call(s32[3]{0:T(128)S(1)} %pad_add_fusion.off_ref.role_ref, bf16[256,2048]{1,0:T(8,128)(2,1)} %collective-permute-done.11.x_ref, bf16[2048,3584]{1,0:T(8,128)(2,1)} %gate_hbm.19, bf16[2048,3584]{1,0:T(8,128)(2,1)} %up_hbm.19), custom_call_target="tpu_custom_call" | custom-call | flops 4294967296 | bytes 16777216 | tf_op jit(solution)/shard_map/pallas_call | solution.py:65
  96.2 8.8 %collective-permute-done.12.refs_1_ = bf16[256,2048]{1,0:T(8,128)(2,1)S(1)} collective-permute-done((bf16[256,2048]{1,0:T(8,128)(2,1)S(1)}, bf16[256,2048]{1,0:T(8,128)(2,1)S(1)}, u32[]{:S(2)}, u32[]{:S(2)}) %collective-permute-start.12) | collective-permute-done | bytes 1048608 | tf_op jit(solution)/shard_map/ppermute | solution.py:355
  105.0 2.7 shard_map.68
  107.7 3.5 collective-permute-start.14
  112.3 2.6 collective-permute-start.10
  115.0 9.4 %shard_map.66 = (bf16[256,1536]{1,0:T(8,128)(2,1)S(1)}, bf16[256,1536]{1,0:T(8,128)(2,1)S(1)}) custom-call(s32[3]{0:T(128)S(1)} %pad_add_fusion.off_ref.role_ref, bf16[256,2048]{1,0:T(8,128)(2,1)} %collective-permute-done.11.x_ref, bf16[2048,3584]{1,0:T(8,128)(2,1)} %gate_hbm.19, bf16[2048,3584]{1,0:T(8,128)(2,1)} %up_hbm.19), custom_call_target="tpu_custom_call" | custom-call | flops 3221225472 | bytes 12582912 | tf_op jit(solution)/shard_map/pallas_call | solution.py:65
  127.0 9.1 %collective-permute-done.14.refs_1_.refs_5_ = bf16[256,2560]{1,0:T(8,128)(2,1)S(1)} collective-permute-done((bf16[256,2560]{1,0:T(8,128)(2,1)}, bf16[256,2560]{1,0:T(8,128)(2,1)S(1)}, u32[]{:S(2)}, u32[]{:S(2)}) %collective-permute-start.14) | collective-permute-done | bytes 1310752 | tf_op jit(solution)/shard_map/ppermute | solution.py:355
  136.1 1.7 copy-done.18
  142.2 1.4 shard_map.69
  143.6 1.5 collective-permute-start.17
  146.0 11.1 %shard_map.65 = (bf16[256,2048]{1,0:T(8,128)(2,1)S(1)}, bf16[256,2048]{1,0:T(8,128)(2,1)}) custom-call(s32[3]{0:T(128)S(1)} %pad_add_fusion.off_ref.role_ref, bf16[256,2048]{1,0:T(8,128)(2,1)} %collective-permute-done.10.x_ref, bf16[2048,3584]{1,0:T(8,128)(2,1)} %gate_hbm.19, bf16[2048,3584]{1,0:T(8,128)(2,1)} %up_hbm.19), custom_call_target="tpu_custom_call" | custom-call | flops 4294967296 | bytes 16777216 | tf_op jit(solution)/shard_map/pallas_call | solution.py:65
  157.0 12.6 %collective-permute-done.17.refs_1_.refs_2_ = bf16[256,2560]{1,0:T(8,128)(2,1)S(1)} collective-permute-done((bf16[256,2560]{1,0:T(8,128)(2,1)S(1)}, bf16[256,2560]{1,0:T(8,128)(2,1)S(1)}, u32[]{:S(2)}, u32[]{:S(2)}) %collective-permute-start.17) | collective-permute-done | bytes 1310752 | tf_op jit(solution)/shard_map/ppermute | solution.py:355
  169.7 2.9 shard_map.70
  172.6 3.6 collective-permute-start.19
  177.0 1.6 collective-permute-start.20
  178.6 2.1 collective-permute-done.20
  180.8 9.5 %shard_map.64 = (bf16[256,1536]{1,0:T(8,128)(2,1)S(1)}, bf16[256,1536]{1,0:T(8,128)(2,1)S(1)}) custom-call(s32[3]{0:T(128)S(1)} %pad_add_fusion.off_ref.role_ref, bf16[256,2048]{1,0:T(8,128)(2,1)} %collective-permute-done.10.x_ref, bf16[2048,3584]{1,0:T(8,128)(2,1)} %gate_hbm.19, bf16[2048,3584]{1,0:T(8,128)(2,1)} %up_hbm.19), custom_call_target="tpu_custom_call" | custom-call | flops 3221225472 | bytes 12582912 | tf_op jit(solution)/shard_map/pallas_call | solution.py:65
  190.4 12.0 %collective-permute-done.19.refs_1_.refs_6_.refs_5_ = bf16[256,2816]{1,0:T(8,128)(2,1)S(1)} collective-permute-done((bf16[256,2816]{1,0:T(8,128)(2,1)}, bf16[256,2816]{1,0:T(8,128)(2,1)S(1)}, u32[]{:S(2)}, u32[]{:S(2)}) %collective-permute-start.19) | collective-permute-done | bytes 1441824 | tf_op jit(solution)/shard_map/ppermute | solution.py:355
  202.4 1.4 shard_map.71
  204.7 4.9 %collective-permute-start.22 = (bf16[256,2560]{1,0:T(8,128)(2,1)S(1)}, bf16[256,2560]{1,0:T(8,128)(2,1)S(1)}, u32[]{:S(2)}, u32[]{:S(2)}) collective-permute-start(bf16[256,2560]{1,0:T(8,128)(2,1)S(1)} %get-tuple-element.149.refs_0_), channel_id=1, source_target_pairs={{0,1},{2,3},{1,0},{3,2},{4,5},{6,7},{5,4},{7,6},{8,9},{10,11},{9,8... | collective-permute-start | bytes 3932168 | tf_op jit(solution)/shard_map/ppermute | solution.py:355
  209.6 6.2 %shard_map.56 = (bf16[256,1024]{1,0:T(8,128)(2,1)S(1)}, bf16[256,1024]{1,0:T(8,128)(2,1)S(1)}) custom-call(s32[3]{0:T(128)S(1)} %pad_add_fusion.off_ref.role_ref, bf16[256,2048]{1,0:T(8,128)(2,1)} %copy-done, bf16[2048,3584]{1,0:T(8,128)(2,1)} %gate_hbm.19, bf16[2048,3584]{1,0:T(8,128)(2,1)} %up_hbm.19), custom_call_target="tpu_custom_call" | custom-call | flops 2147483648 | bytes 8388608 | tf_op jit(solution)/shard_map/pallas_call | solution.py:65
  215.9 10.3 %shard_map.73.refs_4_ = f32[256,2048]{1,0:T(8,128)} custom-call(s32[3]{0:T(128)S(1)} %pad_add_fusion.off_ref.role_ref, bf16[3584,2048]{1,0:T(8,128)(2,1)} %weight_hbm.13, bf16[256,2048]{1,0:T(8,128)(2,1)S(1)} %copy-done.47, bf16[256,2048]{1,0:T(8,128)(2,1)} %copy-done.16, bf16[256,2560]{1,0:T(8,128)(2,1)} %copy-done.5, bf16[256,2048]{1,0:T(8,128)(2,1)} %copy-done.15, ...), custom_call_target="tpu_custom_call" | custom-call | flops 2147483648 | bytes 8388608 | tf_op jit(solution)/shard_map/pallas_call | solution.py:119
  226.2 5.7 %collective-permute-done.22.refs_1_.refs_2_ = bf16[256,2560]{1,0:T(8,128)(2,1)S(1)} collective-permute-done((bf16[256,2560]{1,0:T(8,128)(2,1)S(1)}, bf16[256,2560]{1,0:T(8,128)(2,1)S(1)}, u32[]{:S(2)}, u32[]{:S(2)}) %collective-permute-start.22) | collective-permute-done | bytes 1310752 | tf_op jit(solution)/shard_map/ppermute | solution.py:355
  231.9 2.9 shard_map.72
  234.8 2.4 collective-permute-start.24
  238.7 3.7 shard_map.55
  243.9 18.0 %collective-permute-done.24.refs_1_.refs_6_.refs_5_ = bf16[256,2816]{1,0:T(8,128)(2,1)S(1)} collective-permute-done((bf16[256,2816]{1,0:T(8,128)(2,1)}, bf16[256,2816]{1,0:T(8,128)(2,1)S(1)}, u32[]{:S(2)}, u32[]{:S(2)}) %collective-permute-start.24) | collective-permute-done | bytes 1441824 | tf_op jit(solution)/shard_map/ppermute | solution.py:355
  261.9 1.7 copy-done.26
  266.8 1.4 shard_map.74
  268.2 1.3 collective-permute-start.27
  270.3 25.5 %collective-permute-done.27.refs_1_.refs_2_ = bf16[256,2560]{1,0:T(8,128)(2,1)S(1)} collective-permute-done((bf16[256,2560]{1,0:T(8,128)(2,1)S(1)}, bf16[256,2560]{1,0:T(8,128)(2,1)S(1)}, u32[]{:S(2)}, u32[]{:S(2)}) %collective-permute-start.27) | collective-permute-done | bytes 1310752 | tf_op jit(solution)/shard_map/ppermute | solution.py:355
  297.2 1.3 collective-permute-start.29
  299.2 17.2 %collective-permute-done.29.refs_1_.refs_6_ = bf16[256,1792]{1,0:T(8,128)(2,1)S(1)} collective-permute-done((bf16[256,1792]{1,0:T(8,128)(2,1)S(1)}, bf16[256,1792]{1,0:T(8,128)(2,1)S(1)}, u32[]{:S(2)}, u32[]{:S(2)}) %collective-permute-start.29) | collective-permute-done | bytes 917536 | tf_op jit(solution)/shard_map/ppermute | solution.py:355
  319.6 12.6 %shard_map.83 = bf16[256,2048]{1,0:T(8,128)(2,1)S(1)} custom-call(s32[3]{0:T(128)S(1)} %pad_add_fusion.off_ref.role_ref, bf16[3584,2048]{1,0:T(8,128)(2,1)} %weight_hbm.13, bf16[256,2560]{1,0:T(8,128)(2,1)} %copy-done.41, bf16[256,2560]{1,0:T(8,128)(2,1)} %copy-done.5, bf16[256,2560]{1,0:T(8,128)(2,1)} %copy-done.7, bf16[256,2560]{1,0:T(8,128)(2,1)} %copy-done.12, ...), custom_call_target="tpu_custom_call" | custom-call | flops 3758096384 | bytes 14680064 | tf_op jit(solution)/shard_map/pallas_call | solution.py:119
  335.2 2.3 collective-permute-start.33
  338.1 12.5 %shard_map.84 = bf16[256,2048]{1,0:T(8,128)(2,1)} custom-call(s32[3]{0:T(128)S(1)} %pad_add_fusion.off_ref.role_ref, bf16[3584,2048]{1,0:T(8,128)(2,1)} %weight_hbm.13, bf16[256,2560]{1,0:T(8,128)(2,1)} %copy-done.42, bf16[256,2560]{1,0:T(8,128)(2,1)} %copy-done.7, bf16[256,2560]{1,0:T(8,128)(2,1)} %copy-done.6, bf16[256,2560]{1,0:T(8,128)(2,1)} %copy-done.13, ...), custom_call_target="tpu_custom_call" | custom-call | flops 3758096384 | bytes 14680064 | tf_op jit(solution)/shard_map/pallas_call | solution.py:119
  350.6 1.5 collective-permute-start.39
  352.1 8.3 %shard_map.79.refs_4_ = f32[256,2048]{1,0:T(8,128)} custom-call(s32[3]{0:T(128)S(1)} %pad_add_fusion.off_ref.role_ref, bf16[3584,2048]{1,0:T(8,128)(2,1)} %weight_hbm.13, bf16[256,2560]{1,0:T(8,128)(2,1)} %copy-done.43, bf16[256,2560]{1,0:T(8,128)(2,1)} %copy-done.6, bf16[256,1536]{1,0:T(8,128)(2,1)S(1)} %collective-permute-done.31.refs_1_.refs_2_, ...), custom_call_target="tpu_custom_call" | custom-call | flops 2147483648 | bytes 8388608 | tf_op jit(solution)/shard_map/pallas_call | solution.py:119
  360.9 6.7 %shard_map.85 = bf16[256,2048]{1,0:T(8,128)(2,1)} custom-call(s32[3]{0:T(128)S(1)} %pad_add_fusion.off_ref.role_ref, bf16[3584,2048]{1,0:T(8,128)(2,1)} %weight_hbm.13, bf16[256,1792]{1,0:T(8,128)(2,1)S(1)} %get-tuple-element.167.refs_0_, bf16[256,1792]{1,0:T(8,128)(2,1)} %copy-done.8, bf16[256,768]{1,0:T(8,128)(2,1)S(1)} %collective-permute-done.33.refs_1_.refs_2_, ...), custom_call_target="tpu_custom_call" | custom-call | flops 1610612736 | bytes 6291456 | tf_op jit(solution)/shard_map/pallas_call | solution.py:119
  367.6 1.9 collective-permute-start.40
  369.5 3.5 collective-permute-start.36
  374.3 3.1 collective-permute-done.36.refs_2_
  377.4 3.2 collective-permute-start.37
  380.6 6.1 %shard_map.81.refs_4_ = f32[256,2048]{1,0:T(8,128)} custom-call(s32[3]{0:T(128)S(1)} %pad_add_fusion.off_ref.role_ref, bf16[3584,2048]{1,0:T(8,128)(2,1)} %weight_hbm.13, bf16[256,1536]{1,0:T(8,128)(2,1)S(1)} %get-tuple-element.171.refs_0_, bf16[256,1536]{1,0:T(8,128)(2,1)} %copy-done.9, bf16[256,512]{1,0:T(8,128)(2,1)S(1)} %collective-permute-done.36.refs_2_, ...), custom_call_target="tpu_custom_call" | custom-call | flops 1073741824 | bytes 4194304 | tf_op jit(solution)/shard_map/pallas_call | solution.py:119
  386.7 5.4 %shard_map.82 = f32[256,2048]{1,0:T(8,128)} custom-call(s32[3]{0:T(128)S(1)} %pad_add_fusion.off_ref.role_ref, bf16[3584,2048]{1,0:T(8,128)(2,1)} %weight_hbm.13, bf16[256,768]{1,0:T(8,128)(2,1)S(1)} %get-tuple-element.175.refs_0_, bf16[256,768]{1,0:T(8,128)(2,1)S(1)} %collective-permute-done.33.refs_1_.refs_2_, ...), custom_call_target="tpu_custom_call" | custom-call | flops 536870912 | bytes 2097152 | tf_op jit(solution)/shard_map/pallas_call | solution.py:119
  392.1 2.3 convert_add_fusion
  394.5 1.9 collective-permute-done.41
  (171 shorter events, 36.4 us)
Async XLA Ops:
  1.3 3.3 collective-permute-start
  1.8 4.5 %collective-permute-start.2 = (f32[1,128]{1,0:T(1,128)S(1)}, f32[1,128]{1,0:T(1,128)S(1)}, u32[]{:S(2)}, u32[]{:S(2)}) collective-permute-start(f32[1,128]{1,0:T(1,128)S(1)} %bitcast.13), channel_id=1, source_target_pairs={{0,1},{1,0},{2,3},{3,2},{4,5},{5,4},{6,7},{7,6},{8,9},{9,8},{10,11... | collective-permute-start | bytes 1544 | tf_op jit(solution)/shard_map/ppermute | solution.py:265
  4.6 38.1 %collective-permute-start.1 = (bf16[256,2048]{1,0:T(8,128)(2,1)S(1)}, bf16[256,2048]{1,0:T(8,128)(2,1)S(1)}, u32[]{:S(2)}, u32[]{:S(2)}) collective-permute-start(bf16[256,2048]{1,0:T(8,128)(2,1)S(1)} %pad_maximum_fusion.x_ref), channel_id=1, source_target_pairs={{0,8},{4,12},{8,0},{12,4},{16,24},{20,28},{24,16},{28,20},{1,9},{5... | collective-permute-start | bytes 3145736 | tf_op jit(solution)/shard_map/ppermute | solution.py:262
  12.6 42.2 %copy-start.37 = (bf16[256,1024]{1,0:T(8,128)(2,1)}, bf16[256,1024]{1,0:T(8,128)(2,1)S(1)}, u32[]{:S(2)}) copy-start(bf16[256,1024]{1,0:T(8,128)(2,1)S(1)} %get-tuple-element.109.refs_1_.refs_0_) | copy-start | bytes 1572868
  12.6 13.8 %collective-permute-start.3 = (bf16[256,1024]{1,0:T(8,128)(2,1)S(1)}, bf16[256,1024]{1,0:T(8,128)(2,1)S(1)}, u32[]{:S(2)}, u32[]{:S(2)}) collective-permute-start(bf16[256,1024]{1,0:T(8,128)(2,1)S(1)} %get-tuple-element.113.refs_1_), channel_id=1, source_target_pairs={{0,1},{2,3},{1,0},{3,2},{4,5},{6,7},{5,4},{7,6},{8,9},{10,11},{9,8... | collective-permute-start | bytes 1572872 | tf_op jit(solution)/shard_map/ppermute | solution.py:355
  26.9 27.8 %collective-permute-start.4 = (bf16[256,1024]{1,0:T(8,128)(2,1)S(1)}, bf16[256,1024]{1,0:T(8,128)(2,1)S(1)}, u32[]{:S(2)}, u32[]{:S(2)}) collective-permute-start(bf16[256,1024]{1,0:T(8,128)(2,1)S(1)} %shard_map.60), channel_id=1, source_target_pairs={{1,2},{2,1},{5,6},{6,5},{9,10},{10,9},{13,14},{14,13},{17,18},{18,... | collective-permute-start | bytes 1572872 | tf_op jit(solution)/shard_map/ppermute | solution.py:355
  27.6 27.1 %collective-permute-start.5 = (bf16[256,1024]{1,0:T(8,128)(2,1)S(1)}, bf16[256,1024]{1,0:T(8,128)(2,1)S(1)}, u32[]{:S(2)}, u32[]{:S(2)}) collective-permute-start(bf16[256,1024]{1,0:T(8,128)(2,1)S(1)} %get-tuple-element.115.refs_0_.refs_3_), channel_id=1, source_target_pairs={{0,1},{2,3},{1,0},{3,2},{4,5},{6,7},{5,4},{7,6},{8,9},{10,11},{9,8... | collective-permute-start | bytes 1572872 | tf_op jit(solution)/shard_map/ppermute | solution.py:355
  32.2 10.5 %collective-permute-start.6 = (f32[1,128]{1,0:T(1,128)S(1)}, f32[1,128]{1,0:T(1,128)S(1)}, u32[]{:S(2)}, u32[]{:S(2)}) collective-permute-start(f32[1,128]{1,0:T(1,128)S(1)} %bitcast_add_fusion), channel_id=1, source_target_pairs={{0,2},{1,3},{2,0},{3,1},{4,6},{5,7},{6,4},{7,5},{8,10},{9,11},{10,... | collective-permute-start | bytes 1544 | tf_op jit(solution)/shard_map/ppermute | solution.py:265
  56.6 23.1 %collective-permute-start.7 = (bf16[256,2048]{1,0:T(8,128)(2,1)}, bf16[256,2048]{1,0:T(8,128)(2,1)}, u32[]{:S(2)}, u32[]{:S(2)}) collective-permute-start(bf16[256,2048]{1,0:T(8,128)(2,1)} %get-tuple-element.119), channel_id=1, source_target_pairs={{0,1},{2,3},{1,0},{3,2},{4,5},{6,7},{5,4},{7,6},{8,9},{10,11},{9,8... | collective-permute-start | bytes 3145736 | tf_op jit(solution)/shard_map/ppermute | solution.py:355
  58.6 26.5 %collective-permute-start.11 = (bf16[256,2048]{1,0:T(8,128)(2,1)S(1)}, bf16[256,2048]{1,0:T(8,128)(2,1)}, u32[]{:S(2)}, u32[]{:S(2)}) collective-permute-start(bf16[256,2048]{1,0:T(8,128)(2,1)S(1)} %copy-done.1), channel_id=1, source_target_pairs={{0,16},{4,20},{8,24},{12,28},{16,0},{20,4},{24,8},{28,12},{1,17},{... | collective-permute-start | bytes 3145736 | tf_op jit(solution)/shard_map/ppermute | solution.py:262
  60.2 11.9 %collective-permute-start.9 = (bf16[256,1024]{1,0:T(8,128)(2,1)}, bf16[256,1024]{1,0:T(8,128)(2,1)}, u32[]{:S(2)}, u32[]{:S(2)}) collective-permute-start(bf16[256,1024]{1,0:T(8,128)(2,1)} %get-tuple-element.123), channel_id=1, source_target_pairs={{1,2},{2,1},{5,6},{6,5},{9,10},{10,9},{13,14},{14,13},{17,18},{18,... | collective-permute-start | bytes 1572872 | tf_op jit(solution)/shard_map/ppermute | solution.py:355
  61.6 10.3 %collective-permute-start.8 = (f32[1,128]{1,0:T(1,128)S(1)}, f32[1,128]{1,0:T(1,128)S(1)}, u32[]{:S(2)}, u32[]{:S(2)}) collective-permute-start(f32[1,128]{1,0:T(1,128)S(1)} %add_rsqrt_fusion), channel_id=1, source_target_pairs={{0,4},{4,0},{8,12},{12,8},{16,20},{20,16},{24,28},{28,24},{1,5},{5... | collective-permute-start | bytes 1544 | tf_op jit(solution)/shard_map/ppermute | solution.py:262
  82.9 13.3 %copy-start.46 = (bf16[256,2048]{1,0:T(8,128)(2,1)}, bf16[256,2048]{1,0:T(8,128)(2,1)S(1)}, u32[]{:S(2)}) copy-start(bf16[256,2048]{1,0:T(8,128)(2,1)S(1)} %get-tuple-element.134.refs_0_) | copy-start | bytes 3145732
  82.9 22.0 %copy-start.17 = (bf16[256,2048]{1,0:T(8,128)(2,1)S(1)}, bf16[256,2048]{1,0:T(8,128)(2,1)}, u32[]{:S(2)}) copy-start(bf16[256,2048]{1,0:T(8,128)(2,1)} %get-tuple-element.133.refs_4_.refs_0_) | copy-start | bytes 3145732
  82.9 22.0 %collective-permute-start.12 = (bf16[256,2048]{1,0:T(8,128)(2,1)S(1)}, bf16[256,2048]{1,0:T(8,128)(2,1)S(1)}, u32[]{:S(2)}, u32[]{:S(2)}) collective-permute-start(bf16[256,2048]{1,0:T(8,128)(2,1)S(1)} %get-tuple-element.134.refs_0_), channel_id=1, source_target_pairs={{0,1},{2,3},{1,0},{3,2},{4,5},{6,7},{5,4},{7,6},{8,9},{10,11},{9,8... | collective-permute-start | bytes 3145736 | tf_op jit(solution)/shard_map/ppermute | solution.py:355
  84.4 20.5 %collective-permute-start.13 = (bf16[256,2048]{1,0:T(8,128)(2,1)S(1)}, bf16[256,2048]{1,0:T(8,128)(2,1)S(1)}, u32[]{:S(2)}, u32[]{:S(2)}) collective-permute-start(bf16[256,2048]{1,0:T(8,128)(2,1)S(1)} %get-tuple-element.136), channel_id=1, source_target_pairs={{1,2},{2,1},{5,6},{6,5},{9,10},{10,9},{13,14},{14,13},{17,18},{18,... | collective-permute-start | bytes 3145736 | tf_op jit(solution)/shard_map/ppermute | solution.py:355
  107.7 28.4 %collective-permute-start.14 = (bf16[256,2560]{1,0:T(8,128)(2,1)}, bf16[256,2560]{1,0:T(8,128)(2,1)S(1)}, u32[]{:S(2)}, u32[]{:S(2)}) collective-permute-start(bf16[256,2560]{1,0:T(8,128)(2,1)} %get-tuple-element.137.refs_4_), channel_id=1, source_target_pairs={{0,1},{2,3},{1,0},{3,2},{4,5},{6,7},{5,4},{7,6},{8,9},{10,11},{9,8... | collective-permute-start | bytes 3932168 | tf_op jit(solution)/shard_map/ppermute | solution.py:355
  111.2 15.8 %collective-permute-start.16 = (bf16[256,2048]{1,0:T(8,128)(2,1)}, bf16[256,2048]{1,0:T(8,128)(2,1)S(1)}, u32[]{:S(2)}, u32[]{:S(2)}) collective-permute-start(bf16[256,2048]{1,0:T(8,128)(2,1)} %get-tuple-element.140), channel_id=1, source_target_pairs={{1,2},{2,1},{5,6},{6,5},{9,10},{10,9},{13,14},{14,13},{17,18},{18,... | collective-permute-start | bytes 3145736 | tf_op jit(solution)/shard_map/ppermute | solution.py:355
  111.9 14.2 %collective-permute-start.15 = (f32[2,128]{1,0:T(2,128)S(1)}, f32[2,128]{1,0:T(2,128)S(1)}, u32[]{:S(2)}, u32[]{:S(2)}) collective-permute-start(f32[2,128]{1,0:T(2,128)S(1)} %pad_maximum_fusion.1), channel_id=1, source_target_pairs={{0,8},{4,12},{8,0},{12,4},{16,24},{20,28},{24,16},{28,20},{1,9},{5... | collective-permute-start | bytes 3080 | tf_op jit(solution)/shard_map/ppermute | solution.py:262
  112.3 33.7 %collective-permute-start.10 = (bf16[256,2048]{1,0:T(8,128)(2,1)S(1)}, bf16[256,2048]{1,0:T(8,128)(2,1)}, u32[]{:S(2)}, u32[]{:S(2)}) collective-permute-start(bf16[256,2048]{1,0:T(8,128)(2,1)S(1)} %copy-done.1), channel_id=1, source_target_pairs={{0,24},{4,28},{8,16},{12,20},{16,8},{20,12},{24,0},{28,4},{1,25},{... | collective-permute-start | bytes 3145736 | tf_op jit(solution)/shard_map/ppermute | solution.py:262
  127.0 16.6 %copy-start.15 = (bf16[256,2048]{1,0:T(8,128)(2,1)}, bf16[256,2048]{1,0:T(8,128)(2,1)S(1)}, u32[]{:S(2)}) copy-start(bf16[256,2048]{1,0:T(8,128)(2,1)S(1)} %collective-permute-done.16.refs_4_.refs_3_) | copy-start | bytes 3145732
  143.6 13.4 %copy-start.41 = (bf16[256,2560]{1,0:T(8,128)(2,1)}, bf16[256,2560]{1,0:T(8,128)(2,1)S(1)}, u32[]{:S(2)}) copy-start(bf16[256,2560]{1,0:T(8,128)(2,1)S(1)} %get-tuple-element.141.refs_0_) | copy-start | bytes 3932164
  143.6 26.0 %collective-permute-start.17 = (bf16[256,2560]{1,0:T(8,128)(2,1)S(1)}, bf16[256,2560]{1,0:T(8,128)(2,1)S(1)}, u32[]{:S(2)}, u32[]{:S(2)}) collective-permute-start(bf16[256,2560]{1,0:T(8,128)(2,1)S(1)} %get-tuple-element.141.refs_0_), channel_id=1, source_target_pairs={{0,1},{2,3},{1,0},{3,2},{4,5},{6,7},{5,4},{7,6},{8,9},{10,11},{9,8... | collective-permute-start | bytes 3932168 | tf_op jit(solution)/shard_map/ppermute | solution.py:355
  145.1 24.6 %copy-start.19 = (bf16[256,2048]{1,0:T(8,128)(2,1)S(1)}, bf16[256,2048]{1,0:T(8,128)(2,1)}, u32[]{:S(2)}) copy-start(bf16[256,2048]{1,0:T(8,128)(2,1)} %get-tuple-element.131.refs_5_.refs_0_) | copy-start | bytes 3145732
  145.1 24.6 %copy-start.29 = (bf16[256,1536]{1,0:T(8,128)(2,1)S(1)}, bf16[256,1536]{1,0:T(8,128)(2,1)}, u32[]{:S(2)}) copy-start(bf16[256,1536]{1,0:T(8,128)(2,1)} %copy-done.27) | copy-start | bytes 2359300
  145.1 24.6 %copy-start.32 = (bf16[256,1536]{1,0:T(8,128)(2,1)S(1)}, bf16[256,1536]{1,0:T(8,128)(2,1)}, u32[]{:S(2)}) copy-start(bf16[256,1536]{1,0:T(8,128)(2,1)} %copy-done.30) | copy-start | bytes 2359300
  145.1 24.6 %copy-start.45 = (f32[256,1]{1,0:T(8,128)S(1)}, f32[256,1]{1,0:T(8,128)}, u32[]{:S(2)}) copy-start(f32[256,1]{1,0:T(8,128)} %copy.8.refs_2_) | copy-start | bytes 3076
  145.1 24.6 %collective-permute-start.18 = (bf16[256,2560]{1,0:T(8,128)(2,1)S(1)}, bf16[256,2560]{1,0:T(8,128)(2,1)S(1)}, u32[]{:S(2)}, u32[]{:S(2)}) collective-permute-start(bf16[256,2560]{1,0:T(8,128)(2,1)S(1)} %get-tuple-element.143), channel_id=1, source_target_pairs={{1,2},{2,1},{5,6},{6,5},{9,10},{10,9},{13,14},{14,13},{17,18},{18,... | collective-permute-start | bytes 3932168 | tf_op jit(solution)/shard_map/ppermute | solution.py:355
  157.0 15.6 %copy-start.23 = (bf16[256,2048]{1,0:T(8,128)(2,1)}, bf16[256,2048]{1,0:T(8,128)(2,1)S(1)}, u32[]{:S(2)}) copy-start(bf16[256,2048]{1,0:T(8,128)(2,1)S(1)} %get-tuple-element.142.refs_3_.refs_6_) | copy-start | bytes 3145732
  172.6 29.8 %collective-permute-start.19 = (bf16[256,2816]{1,0:T(8,128)(2,1)}, bf16[256,2816]{1,0:T(8,128)(2,1)S(1)}, u32[]{:S(2)}, u32[]{:S(2)}) collective-permute-start(bf16[256,2816]{1,0:T(8,128)(2,1)} %get-tuple-element.144.refs_4_), channel_id=1, source_target_pairs={{0,1},{2,3},{1,0},{3,2},{4,5},{6,7},{5,4},{7,6},{8,9},{10,11},{9,8... | collective-permute-start | bytes 4325384 | tf_op jit(solution)/shard_map/ppermute | solution.py:355
  176.2 14.1 %collective-permute-start.21 = (bf16[256,2560]{1,0:T(8,128)(2,1)}, bf16[256,2560]{1,0:T(8,128)(2,1)S(1)}, u32[]{:S(2)}, u32[]{:S(2)}) collective-permute-start(bf16[256,2560]{1,0:T(8,128)(2,1)} %get-tuple-element.146), channel_id=1, source_target_pairs={{1,2},{2,1},{5,6},{6,5},{9,10},{10,9},{13,14},{14,13},{17,18},{18,... | collective-permute-start | bytes 3932168 | tf_op jit(solution)/shard_map/ppermute | solution.py:355
  177.0 3.6 collective-permute-start.20
  180.8 21.6 %copy-start.20 = (bf16[256,2048]{1,0:T(8,128)(2,1)S(1)}, bf16[256,2048]{1,0:T(8,128)(2,1)}, u32[]{:S(2)}) copy-start(bf16[256,2048]{1,0:T(8,128)(2,1)} %get-tuple-element.131.refs_5_.refs_0_) | copy-start | bytes 3145732
  180.8 21.6 %copy-start.24 = (bf16[256,2048]{1,0:T(8,128)(2,1)S(1)}, bf16[256,2048]{1,0:T(8,128)(2,1)}, u32[]{:S(2)}) copy-start(bf16[256,2048]{1,0:T(8,128)(2,1)} %copy-done.23) | copy-start | bytes 3145732
  180.8 21.6 %copy-start.34 = (bf16[256,1536]{1,0:T(8,128)(2,1)S(1)}, bf16[256,1536]{1,0:T(8,128)(2,1)}, u32[]{:S(2)}) copy-start(bf16[256,1536]{1,0:T(8,128)(2,1)} %copy-done.33) | copy-start | bytes 2359300
  190.3 13.4 %copy-start.35 = (bf16[256,1536]{1,0:T(8,128)(2,1)}, bf16[256,1536]{1,0:T(8,128)(2,1)S(1)}, u32[]{:S(2)}) copy-start(bf16[256,1536]{1,0:T(8,128)(2,1)S(1)} %get-tuple-element.127.refs_5_.refs_0_) | copy-start | bytes 2359300
  190.4 13.4 %copy-start.12 = (bf16[256,2560]{1,0:T(8,128)(2,1)}, bf16[256,2560]{1,0:T(8,128)(2,1)S(1)}, u32[]{:S(2)}) copy-start(bf16[256,2560]{1,0:T(8,128)(2,1)S(1)} %collective-permute-done.21.refs_4_.refs_3_) | copy-start | bytes 3932164
  203.8 28.0 %collective-permute-start.23 = (bf16[256,2816]{1,0:T(8,128)(2,1)S(1)}, bf16[256,2816]{1,0:T(8,128)(2,1)S(1)}, u32[]{:S(2)}, u32[]{:S(2)}) collective-permute-start(bf16[256,2816]{1,0:T(8,128)(2,1)S(1)} %get-tuple-element.151), channel_id=1, source_target_pairs={{1,2},{2,1},{5,6},{6,5},{9,10},{10,9},{13,14},{14,13},{17,18},{18,... | collective-permute-start | bytes 4325384 | tf_op jit(solution)/shard_map/ppermute | solution.py:355
  204.7 27.1 %collective-permute-start.22 = (bf16[256,2560]{1,0:T(8,128)(2,1)S(1)}, bf16[256,2560]{1,0:T(8,128)(2,1)S(1)}, u32[]{:S(2)}, u32[]{:S(2)}) collective-permute-start(bf16[256,2560]{1,0:T(8,128)(2,1)S(1)} %get-tuple-element.149.refs_0_), channel_id=1, source_target_pairs={{0,1},{2,3},{1,0},{3,2},{4,5},{6,7},{5,4},{7,6},{8,9},{10,11},{9,8... | collective-permute-start | bytes 3932168 | tf_op jit(solution)/shard_map/ppermute | solution.py:355
  215.9 16.0 %copy-start.39 = (bf16[256,1024]{1,0:T(8,128)(2,1)}, bf16[256,1024]{1,0:T(8,128)(2,1)S(1)}, u32[]{:S(2)}) copy-start(bf16[256,1024]{1,0:T(8,128)(2,1)S(1)} %get-tuple-element.150.refs_3_.refs_6_) | copy-start | bytes 1572868
  215.9 16.0 %copy-start.25 = (bf16[256,2048]{1,0:T(8,128)(2,1)S(1)}, bf16[256,2048]{1,0:T(8,128)(2,1)}, u32[]{:S(2)}) copy-start(bf16[256,2048]{1,0:T(8,128)(2,1)} %get-tuple-element.128.refs_5_.refs_0_) | copy-start | bytes 3145732
  234.8 27.1 %collective-permute-start.24 = (bf16[256,2816]{1,0:T(8,128)(2,1)}, bf16[256,2816]{1,0:T(8,128)(2,1)S(1)}, u32[]{:S(2)}, u32[]{:S(2)}) collective-permute-start(bf16[256,2816]{1,0:T(8,128)(2,1)} %get-tuple-element.160.refs_4_), channel_id=1, source_target_pairs={{0,1},{2,3},{1,0},{3,2},{4,5},{6,7},{5,4},{7,6},{8,9},{10,11},{9,8... | collective-permute-start | bytes 4325384 | tf_op jit(solution)/shard_map/ppermute | solution.py:355
  237.1 6.7 %collective-permute-start.26 = (bf16[256,2560]{1,0:T(8,128)(2,1)}, bf16[256,2560]{1,0:T(8,128)(2,1)S(1)}, u32[]{:S(2)}, u32[]{:S(2)}) collective-permute-start(bf16[256,2560]{1,0:T(8,128)(2,1)} %get-tuple-element.162), channel_id=1, source_target_pairs={{1,2},{2,1},{5,6},{6,5},{9,10},{10,9},{13,14},{14,13},{17,18},{18,... | collective-permute-start | bytes 3932168 | tf_op jit(solution)/shard_map/ppermute | solution.py:355
  237.9 5.8 %collective-permute-start.25 = (f32[2,128]{1,0:T(2,128)S(1)}, f32[2,128]{1,0:T(2,128)S(1)}, u32[]{:S(2)}, u32[]{:S(2)}) collective-permute-start(f32[2,128]{1,0:T(2,128)S(1)} %pad_maximum_fusion.1), channel_id=1, source_target_pairs={{0,24},{4,28},{8,16},{12,20},{16,8},{20,12},{24,0},{28,4},{1,25},{... | collective-permute-start | bytes 3080 | tf_op jit(solution)/shard_map/ppermute | solution.py:262
  243.9 24.3 %copy-start.13 = (bf16[256,2560]{1,0:T(8,128)(2,1)}, bf16[256,2560]{1,0:T(8,128)(2,1)S(1)}, u32[]{:S(2)}) copy-start(bf16[256,2560]{1,0:T(8,128)(2,1)S(1)} %collective-permute-done.26.refs_4_.refs_3_) | copy-start | bytes 3932164
  268.2 28.9 %copy-start.43 = (bf16[256,2560]{1,0:T(8,128)(2,1)}, bf16[256,2560]{1,0:T(8,128)(2,1)S(1)}, u32[]{:S(2)}) copy-start(bf16[256,2560]{1,0:T(8,128)(2,1)S(1)} %get-tuple-element.165.refs_0_) | copy-start | bytes 3932164
  268.2 27.6 %collective-permute-start.27 = (bf16[256,2560]{1,0:T(8,128)(2,1)S(1)}, bf16[256,2560]{1,0:T(8,128)(2,1)S(1)}, u32[]{:S(2)}, u32[]{:S(2)}) collective-permute-start(bf16[256,2560]{1,0:T(8,128)(2,1)S(1)} %get-tuple-element.165.refs_0_), channel_id=1, source_target_pairs={{0,1},{2,3},{1,0},{3,2},{4,5},{6,7},{5,4},{7,6},{8,9},{10,11},{9,8... | collective-permute-start | bytes 3932168 | tf_op jit(solution)/shard_map/ppermute | solution.py:355
  269.6 0.7 collective-permute-start.28
  295.8 20.6 %copy-start.51 = (bf16[256,512]{1,0:T(8,128)(2,1)S(1)}, bf16[256,512]{1,0:T(8,128)(2,1)}, u32[]{:S(2)}) copy-start(bf16[256,512]{1,0:T(8,128)(2,1)} %copy-done.50) | copy-start | bytes 786436
  297.2 19.2 %collective-permute-start.29 = (bf16[256,1792]{1,0:T(8,128)(2,1)S(1)}, bf16[256,1792]{1,0:T(8,128)(2,1)S(1)}, u32[]{:S(2)}, u32[]{:S(2)}) collective-permute-start(bf16[256,1792]{1,0:T(8,128)(2,1)S(1)} %get-tuple-element.167.refs_0_), channel_id=1, source_target_pairs={{0,1},{2,3},{1,0},{3,2},{4,5},{6,7},{5,4},{7,6},{8,9},{10,11},{9,8... | collective-permute-start | bytes 2752520 | tf_op jit(solution)/shard_map/ppermute | solution.py:355
  298.5 0.7 collective-permute-start.30
  316.4 21.7 %copy-start.8 = (bf16[256,1792]{1,0:T(8,128)(2,1)}, bf16[256,1792]{1,0:T(8,128)(2,1)S(1)}, u32[]{:S(2)}) copy-start(bf16[256,1792]{1,0:T(8,128)(2,1)S(1)} %collective-permute-done.29.refs_1_.refs_6_) | copy-start | bytes 2752516
  317.7 16.3 %collective-permute-start.31 = (bf16[256,1536]{1,0:T(8,128)(2,1)S(1)}, bf16[256,1536]{1,0:T(8,128)(2,1)S(1)}, u32[]{:S(2)}, u32[]{:S(2)}) collective-permute-start(bf16[256,1536]{1,0:T(8,128)(2,1)S(1)} %get-tuple-element.171.refs_0_), channel_id=1, source_target_pairs={{0,1},{2,3},{1,0},{3,2},{4,5},{6,7},{5,4},{7,6},{8,9},{10,11},{9,8... | collective-permute-start | bytes 2359304 | tf_op jit(solution)/shard_map/ppermute | solution.py:355
  318.9 13.7 %collective-permute-start.32 = (bf16[256,768]{1,0:T(8,128)(2,1)S(1)}, bf16[256,768]{1,0:T(8,128)(2,1)S(1)}, u32[]{:S(2)}, u32[]{:S(2)}) collective-permute-start(bf16[256,768]{1,0:T(8,128)(2,1)S(1)} %get-tuple-element.172), channel_id=1, source_target_pairs={{1,2},{2,1},{5,6},{6,5},{9,10},{10,9},{13,14},{14,13},{17,18},{18,... | collective-permute-start | bytes 1179656 | tf_op jit(solution)/shard_map/ppermute | solution.py:355
  332.2 59.9 %collective-permute-start.38 = (bf16[256,2048]{1,0:T(8,128)(2,1)S(1)}, bf16[256,2048]{1,0:T(8,128)(2,1)S(1)}, u32[]{:S(2)}, u32[]{:S(2)}) collective-permute-start(bf16[256,2048]{1,0:T(8,128)(2,1)S(1)} %shard_map.83), channel_id=1, source_target_pairs={{0,8},{4,12},{8,0},{12,4},{16,24},{20,28},{24,16},{28,20},{1,9},{5... | collective-permute-start | bytes 3145736 | tf_op jit(solution)/shard_map/ppermute | solution.py:262
  334.0 18.1 %copy-start.9 = (bf16[256,1536]{1,0:T(8,128)(2,1)}, bf16[256,1536]{1,0:T(8,128)(2,1)S(1)}, u32[]{:S(2)}) copy-start(bf16[256,1536]{1,0:T(8,128)(2,1)S(1)} %collective-permute-done.31.refs_1_.refs_2_) | copy-start | bytes 2359300
  335.2 25.2 %collective-permute-start.33 = (bf16[256,768]{1,0:T(8,128)(2,1)S(1)}, bf16[256,768]{1,0:T(8,128)(2,1)S(1)}, u32[]{:S(2)}, u32[]{:S(2)}) collective-permute-start(bf16[256,768]{1,0:T(8,128)(2,1)S(1)} %get-tuple-element.175.refs_0_), channel_id=1, source_target_pairs={{0,1},{2,3},{1,0},{3,2},{4,5},{6,7},{5,4},{7,6},{8,9},{10,11},{9,8... | collective-permute-start | bytes 1179656 | tf_op jit(solution)/shard_map/ppermute | solution.py:355
  337.4 22.9 %collective-permute-start.34 = (bf16[256,512]{1,0:T(8,128)(2,1)S(1)}, bf16[256,512]{1,0:T(8,128)(2,1)S(1)}, u32[]{:S(2)}, u32[]{:S(2)}) collective-permute-start(bf16[256,512]{1,0:T(8,128)(2,1)S(1)} %get-tuple-element.176), channel_id=1, source_target_pairs={{1,2},{2,1},{5,6},{6,5},{9,10},{10,9},{13,14},{14,13},{17,18},{18,... | collective-permute-start | bytes 786440 | tf_op jit(solution)/shard_map/ppermute | solution.py:355
  350.6 41.5 %collective-permute-start.39 = (bf16[256,2048]{1,0:T(8,128)(2,1)}, bf16[256,2048]{1,0:T(8,128)(2,1)S(1)}, u32[]{:S(2)}, u32[]{:S(2)}) collective-permute-start(bf16[256,2048]{1,0:T(8,128)(2,1)} %shard_map.84), channel_id=1, source_target_pairs={{0,16},{4,20},{8,24},{12,28},{16,0},{20,4},{24,8},{28,12},{1,17},{... | collective-permute-start | bytes 3145736 | tf_op jit(solution)/shard_map/ppermute | solution.py:262
  367.6 24.5 %collective-permute-start.40 = (bf16[256,2048]{1,0:T(8,128)(2,1)}, bf16[256,2048]{1,0:T(8,128)(2,1)S(1)}, u32[]{:S(2)}, u32[]{:S(2)}) collective-permute-start(bf16[256,2048]{1,0:T(8,128)(2,1)} %shard_map.85), channel_id=1, source_target_pairs={{0,24},{4,28},{8,16},{12,20},{16,8},{20,12},{24,0},{28,4},{1,25},{... | collective-permute-start | bytes 3145736 | tf_op jit(solution)/shard_map/ppermute | solution.py:262
  369.5 7.9 %collective-permute-start.36 = (bf16[256,512]{1,0:T(8,128)(2,1)S(1)}, bf16[256,512]{1,0:T(8,128)(2,1)S(1)}, u32[]{:S(2)}, u32[]{:S(2)}) collective-permute-start(bf16[256,512]{1,0:T(8,128)(2,1)S(1)} %get-tuple-element.183), channel_id=1, source_target_pairs={{0,1},{2,3},{1,0},{3,2},{4,5},{6,7},{5,4},{7,6},{8,9},{10,11},{9,8... | collective-permute-start | bytes 786440 | tf_op jit(solution)/shard_map/ppermute | solution.py:355
  373.1 0.7 collective-permute-start.35
  377.4 9.3 %collective-permute-start.37 = (bf16[256,256]{1,0:T(8,128)(2,1)S(1)}, bf16[256,256]{1,0:T(8,128)(2,1)S(1)}, u32[]{:S(2)}, u32[]{:S(2)}) collective-permute-start(bf16[256,256]{1,0:T(8,128)(2,1)S(1)} %shard_map.80), channel_id=1, source_target_pairs={{0,1},{2,3},{1,0},{3,2},{4,5},{6,7},{5,4},{7,6},{8,9},{10,11},{9,8... | collective-permute-start | bytes 393224 | tf_op jit(solution)/shard_map/ppermute | solution.py:355
  394.4 2.0 collective-permute-start.41
  (31 other events, 96.0 us)
